TPU v7x, 128 devices: a whole 4x4x4 slice. The times are simulated.
128 devices in a mesh: grp: 4 (over y), dev: 32 (over x, z, core).
Axes of the slice: x: 4, y: 4, z: 4, core: 2. Of those that a mesh axis runs over, the one named last changes fastest.
Arguments:
- displacement: float32 [3, 64, 32, 32], P(None, 'dev')
- external_force: float32 [3, 64, 32, 32], P(None, 'dev'), may hold values from -6 to 6
- element_sample: int32 [64, 32, 32], P('dev'), may hold values from 0 to 127, as said below
- lame_field: bfloat16 [128, 32, 1024], P('grp', 'dev'), may hold values from 0.5 to 2
- shear_field: bfloat16 [128, 32, 1024], P('grp', 'dev'), may hold values from 0.29882812 to 3
- plastic_steps: int32 [128], replicated, may hold values from 1 to 4
- owner_slot: int32 [128], replicated, may hold values from 0 to 31, as said below
Outputs:
- displacement_next: float32 [3, 64, 32, 32], P(None, 'dev')
- sample_response: float32 [128, 8], P(('grp', 'dev'))
- micro_strain: float32 [6, 128, 32, 1024], P(None, 'grp', 'dev')
Inputs may be any that keep to these rules, and one draw needn't show every extreme that they name: `element_sample`: every value from 0 to 127 is taken by at least one element. `owner_slot`: within each aligned block of 32 RVEs a permutation of 0 to 31; slot s of a block belongs to the block's owner s.
All inputs are finite; a program needn't handle non-finite values.
Results may differ from a plain program's by a relative error of at most 0.0009.
Values may be sent and summed in bfloat16 or wider, within the bound.
A program may use at most 64 MiB of HBM per device.

v0:
```python
import jax
import jax.numpy as jnp
import numpy as np
from jax import lax
from jax.experimental import pallas as pl
from jax.experimental.pallas import tpu as pltpu
from jax.sharding import PartitionSpec as P

VOX = 32
HALF = 512
KMAX = 4
MESH = pl.DeviceIdType.MESH
NEAR = (-2, -1, 1, 2)

shear_ref = 1.65
lame_ref = 1.25
green_ratio = (lame_ref + shear_ref) / (lame_ref + 2.0 * shear_ref)
relax_rate = 0.35
spring_rate = 0.2
wire = jnp.bfloat16
f32 = jnp.float32
bf16 = jnp.bfloat16


def tables():
    n = np.arange(VOX)
    theta = 2.0 * np.pi / VOX
    ky = np.repeat(n, 16)
    kz = np.tile(np.arange(16), VOX)
    yy = np.repeat(n, VOX)
    zz = np.tile(n, VOX)
    k16 = np.arange(16)

    def zeta(z, k):
        angle = theta * (z * k % VOX)
        return (
            np.where(k == 0, 1.0, np.cos(angle)),
            np.where(k == 0, (-1.0) ** z, -np.sin(angle)),
        )

    cy, sy = np.cos(theta * (np.outer(n, ky) % VOX)), np.sin(theta * (np.outer(n, ky) % VOX))
    zr, zi = zeta(n[:, None], kz[None, :])
    cv, sv = np.cos(theta * (np.outer(n, yy) % VOX)), np.sin(theta * (np.outer(n, yy) % VOX))
    vr, vi = zeta(zz[None, :], k16[:, None])
    c, s = np.cos(theta * (np.outer(n, n) % VOX)), np.sin(theta * (np.outer(n, n) % VOX))
    x = np.block([[c, s], [-s, c]])

    def wave(k):
        return np.where(k % 16 == 0, 0.0, np.sin(theta * k))

    one = np.ones((VOX, HALF))
    xx, xy, xz = wave(n)[:, None] * one, wave(ky)[None] * one, wave(kz)[None] * one
    square = xx * xx + xy * xy + xz * xz
    inverse = np.where(square > 0, 1.0 / np.where(square > 0, square, 1.0), 0.0)
    weight = np.where(kz == 0, 1.0, 2.0)[None] * one
    scaled = -(1.0 / shear_ref) * inverse * weight / VOX**3
    pairs = (xx * xx, xy * xy, xz * xz, 2 * xy * xz, 2 * xx * xz, 2 * xx * xy)
    spectral = np.stack([scaled] + [green_ratio * p * inverse for p in pairs])
    to = lambda a: np.asarray(a, np.float32)
    return (
        to(np.stack([cy, sy, zr, zi])),
        to(np.stack([cv, sv])),
        to(np.stack([vr, vi])),
        to(np.stack([x, x.T])),
        to(spectral),
    )


def split(a):
    high = a.astype(bf16)
    return high, (a - high.astype(f32)).astype(bf16)


def mm(a, b):
    return jnp.dot(a, b, preferred_element_type=f32)


def product(a, b):
    ah, al = split(a)
    bh, bl = split(b)
    return mm(ah, bh) + (mm(al, bh) + mm(ah, bl))


def lane_of(shape):
    return lax.broadcasted_iota(jnp.int32, shape, len(shape) - 1)


def row_of(shape):
    return lax.broadcasted_iota(jnp.int32, shape, len(shape) - 2)


def roll(a, shift, axis):
    return pltpu.roll(a, shift % a.shape[axis], axis)


def z_up(v):
    return jnp.where(lane_of(v.shape) % VOX == VOX - 1, 0.0, roll(v, -1, 2))


def z_down(v):
    return jnp.where(lane_of(v.shape) % VOX == 0, 0.0, roll(v, 1, 2))


def y_up(v):
    moved = roll(v, -VOX, 2)
    next_row = jnp.where(row_of(v.shape) == 7, 0.0, roll(moved, -1, 1))
    return jnp.where(lane_of(v.shape) < 96, moved, next_row)


def y_down(v):
    moved = roll(v, VOX, 2)
    last_row = jnp.where(row_of(v.shape) == 0, 0.0, roll(moved, 1, 1))
    return jnp.where(lane_of(v.shape) >= VOX, moved, last_row)


def zc(v):
    lane = lane_of(v.shape) % VOX
    up = jnp.where(lane == VOX - 1, roll(v, 31, 1), roll(v, -1, 1))
    down = jnp.where(lane == 0, roll(v, -31, 1), roll(v, 1, 1))
    return 0.5 * (up - down)


def yc(v):
    lane = lane_of(v.shape)
    up = roll(v, -VOX, 1)
    up = jnp.where(lane < 96, up, roll(up, -1, 0))
    down = roll(v, VOX, 1)
    down = jnp.where(lane >= VOX, down, roll(down, 1, 0))
    return 0.5 * (up - down)


def strain_of(fields):
    slopes = []
    for w in fields:
        up = z_up(w)
        mz, dz = 0.5 * (w + up), up - w
        moved = y_up(mz)
        a, b = 0.5 * (mz + moved), moved - mz
        c = 0.5 * (dz + y_up(dz))
        slopes.append((a[1:] - a[:-1], 0.5 * (b[1:] + b[:-1]), 0.5 * (c[1:] + c[:-1])))
    x, y, z = slopes
    return (
        x[0],
        y[1],
        z[2],
        0.5 * (z[1] + y[2]),
        0.5 * (z[0] + x[2]),
        0.5 * (y[0] + x[1]),
    )


def force_of(stress):
    xx, yy, zz, yz, xz, xy = stress
    result = []
    for along_x, along_y, along_z in ((xx, xy, xz), (xy, yy, yz), (xz, yz, zz)):
        smooth_x = 0.5 * (along_x + z_down(along_x))
        first = 0.5 * (smooth_x + y_down(smooth_x))
        smooth_y = 0.5 * (along_y + z_down(along_y))
        slope_z = z_down(along_z) - along_z
        rest = (y_down(smooth_y) - smooth_y) + 0.5 * (slope_z + y_down(slope_z))
        result.append((first[:-1] - first[1:]) + 0.5 * (rest[1:] + rest[:-1]))
    return result


def stress_of(strain, lame, shear):
    spread = lame * (strain[0] + strain[1] + strain[2])
    twice = 2.0 * shear
    return [twice * e + spread for e in strain[:3]] + [twice * e for e in strain[3:]]


def norm_of(d):
    return d[0] * d[0] + d[1] * d[1] + d[2] * d[2] + 2.0 * (d[3] * d[3] + d[4] * d[4] + d[5] * d[5])


def relaxed(mu, size, rates):
    base = mu * mu * size
    scale = jnp.ones_like(mu)
    for rate in rates:
        f = base * scale * scale
        scale = scale * (1.0 - rate * (f / (1.0 + f)))
    return scale, base * scale * scale


def kernel(
    steps_ref, slot_ref, disp_ref, force_ref, samp_ref, mod_ref,
    wt_ref, vt_ref, vz_ref, x_ref, spec_ref,
    disp_out, row_out, micro_out,
    nb_disp, nb_force, nb_samp, modbuf, part, partbuf, strainrow,
    wh, wl, vh, vl, field, pot, disp_u, flu, flubuf,
    rowbuf, joined, respbuf, moment, momentbuf,
    near_send, near_recv, mod_send, mod_recv, part_send, part_recv,
    y_send, y_recv, resp_send, resp_recv, flu_send, flu_recv, mom_send, mom_recv,
):
    me = lax.axis_index("dev")
    group = lax.axis_index("grp")
    count = disp_ref.shape[1]

    def peer_of(i):
        return lax.rem(me + i, 32)

    barrier = pltpu.get_barrier_semaphore()

    @pl.loop(1, 32)
    def _(i):
        pl.semaphore_signal(barrier, inc=1, device_id={"dev": peer_of(i)}, device_id_type=MESH)

    for i in range(1, 4):
        pl.semaphore_signal(
            barrier, inc=1, device_id={"grp": lax.rem(group + i, 4)}, device_id_type=MESH
        )

    part[...] = jnp.zeros_like(part)

    @pl.loop(0, 32)
    def _(y):
        c, s = wt_ref[0, pl.ds(y, 1), :], wt_ref[1, pl.ds(y, 1), :]
        zr, zi = wt_ref[2], wt_ref[3]
        rows = pl.ds(pl.multiple_of(y * 32, 32), 32)
        for k, block in enumerate((c * zr + s * zi, c * zi - s * zr)):
            high, low = split(block)
            wh[rows, pl.ds(k * HALF, HALF)] = high
            wl[rows, pl.ds(k * HALF, HALF)] = low

    pl.semaphore_wait(barrier, 34)

    def near_copies(source, target, k):
        out = []
        for o, offset in enumerate(NEAR):
            out.append(
                pltpu.make_async_remote_copy(
                    src_ref=source,
                    dst_ref=target.at[3 - o],
                    send_sem=near_send.at[k, o],
                    recv_sem=near_recv.at[k, 3 - o],
                    device_id={"dev": lax.rem(me + offset + 32, 32)},
                    device_id_type=MESH,
                )
            )
        return out

    near = [
        near_copies(disp_ref, nb_disp, 0),
        near_copies(force_ref, nb_force, 1),
        near_copies(samp_ref, nb_samp, 2),
    ]
    for o in (1, 2, 3, 0):
        near[0][o].start()

    def everyone(source, target, send, recv):
        @pl.loop(1, 32)
        def _(i):
            peer = peer_of(i)
            pltpu.make_async_remote_copy(
                src_ref=source(peer),
                dst_ref=target.at[me],
                send_sem=send,
                recv_sem=recv,
                device_id={"dev": peer},
                device_id_type=MESH,
            ).start()

    def all_arrived(target, recv):
        ref = target.at[pl.ds(0, 31)]
        pltpu.make_async_copy(ref, ref, recv).wait()

    everyone(lambda peer: mod_ref.at[peer], modbuf, mod_send, mod_recv)
    for k in (1, 2):
        for copy in near[k]:
            copy.start()
    modbuf[me] = mod_ref[me]

    pltpu.make_async_copy(disp_ref, nb_disp.at[2], near_recv.at[0, 2]).wait()
    inside_up = (me < 31).astype(f32)
    fields = [
        jnp.concatenate([disp_ref[c], nb_disp[2, c][:1] * inside_up], axis=0) for c in range(3)
    ]
    strain = strain_of(fields)
    one_hots, rows_high, rows_low = [], [], []
    for plane in range(count):
        for c in range(6):
            strainrow[plane, pl.ds(c * 8, 8), :] = strain[c][plane]
        strainrow[plane, pl.ds(48, 8), :] = jnp.ones((8, 128), f32)
        strainrow[plane, pl.ds(56, 8), :] = jnp.zeros((8, 128), f32)
    for plane in range(count):
        sample = samp_ref[plane]
        for s in range(8):
            rows = strainrow[plane, pl.ds(s, 8, stride=8), :]
            high, low = split(rows)
            rows_high.append(high)
            rows_low.append(low)
            hit = jnp.broadcast_to(sample[s : s + 1], (32, 128)) == (
                row_of((32, 128)) + group * 32
            )
            one_hots.append(jnp.where(hit, 1.0, 0.0).astype(bf16))
    one_hot = jnp.concatenate(one_hots, axis=1)

    def against(rows):
        return lax.dot_general(
            one_hot,
            jnp.concatenate(rows, axis=1),
            (((1,), (1,)), ((), ())),
            preferred_element_type=f32,
        )

    sums = against(rows_high) + against(rows_low)
    for r in range(32):
        part[r, :, pl.ds(0, 8)] = sums[r : r + 1]
    everyone(lambda peer: part.at[peer], partbuf, part_send, part_recv)
    partbuf[me] = part[me]

    @pl.loop(0, 32)
    def _(k):
        c, s = vt_ref[0, pl.ds(k, 1), :], vt_ref[1, pl.ds(k, 1), :]
        zr, zi = vz_ref[0], vz_ref[1]
        for p, block in enumerate((c * zr + s * zi, c * zi - s * zr)):
            rows = pl.ds(pl.multiple_of(p * HALF + k * 16, 16), 16)
            high, low = split(block)
            vh[rows, :] = high
            vl[rows, :] = low

    ref = modbuf.at[pl.ds(0, 31)]
    pltpu.make_async_copy(ref, ref, mod_recv).wait()

    def moduli(x):
        both = modbuf[x].astype(f32)
        return both[:8], both[8:]

    def forward(slot):
        rows = jnp.concatenate(
            [field[slot, pl.ds(s, 32, stride=8), :] for s in range(8)], axis=1
        )
        high, low = split(rows)
        both = mm(jnp.concatenate([high, low], axis=0), wh[...])
        plane = both[:32] + (both[32:] + mm(high, wl[...]))
        return product(x_ref[0], jnp.concatenate([plane[:, :HALF], plane[:, HALF:]], axis=0))

    @pl.loop(0, 32)
    def _(x):
        lame, shear = moduli(x)
        field[0, pl.ds(pl.multiple_of(x * 8, 8), 8), :] = lame + (2.0 / 3.0) * shear

    spectrum_a = forward(0)

    ref = partbuf.at[pl.ds(0, 31)]
    pltpu.make_async_copy(ref, ref, part_recv).wait()
    total = jnp.sum(partbuf[...], axis=0)
    lane1 = lane_of((1, 128))

    def pick(row, k):
        return jnp.sum(jnp.where(lane1 == k, row, 0.0), axis=1, keepdims=True)

    members = pick(total, 6)
    load = [pick(total, c) / members for c in range(6)]
    trace = load[0] + load[1] + load[2]
    d = [load[c] - trace / 3.0 if c < 3 else load[c] for c in range(6)]
    own_steps = steps_ref[group * 32 + me]
    rates = [jnp.where(k < own_steps, relax_rate, 0.0).astype(f32) for k in range(KMAX)]
    size = norm_of(d)

    @pl.loop(0, 32)
    def _(x):
        _, shear = moduli(x)
        scale, _ = relaxed(shear, size, rates)
        field[1, pl.ds(pl.multiple_of(x * 8, 8), 8), :] = 2.0 * shear * scale

    spectrum_b = forward(1)
    mix = d[0] * spec_ref[1]
    for c in range(1, 6):
        mix = mix + d[c] * spec_ref[1 + c]
    scaled = spec_ref[0]
    steady = (1.0 - green_ratio) * trace
    phi = [scaled * spectrum_b[:32], scaled * spectrum_b[32:]]
    pressure = [
        scaled * (steady * spectrum_a[:32]) - mix * phi[0],
        scaled * (steady * spectrum_a[32:]) - mix * phi[1],
    ]
    mixed = jnp.concatenate(
        [
            jnp.concatenate([pressure[0], phi[0]], axis=1),
            jnp.concatenate([pressure[1], phi[1]], axis=1),
        ],
        axis=0,
    )
    back = product(x_ref[1], mixed)
    lines = jnp.concatenate(
        [
            jnp.concatenate([back[:32, :HALF], back[32:, :HALF]], axis=1),
            jnp.concatenate([back[:32, HALF:], back[32:, HALF:]], axis=1),
        ],
        axis=0,
    )
    high, low = split(lines)
    both = mm(jnp.concatenate([high, low], axis=0), vh[...])
    space = both[:64] + (both[64:] + mm(high, vl[...]))
    for k in range(2):
        for s in range(8):
            pot[k, pl.ds(s, 32, stride=8), :] = space[k * 32 : k * 32 + 32, s * 128 : s * 128 + 128]

    def at(x):
        return pl.ds(pl.multiple_of(x * 8, 8), 8)

    @pl.loop(0, 32)
    def _(x):
        after, before = lax.rem(x + 1, 32), lax.rem(x + 31, 32)
        p, q = pot[0, at(x), :], pot[1, at(x), :]
        px = 0.5 * (pot[0, at(after), :] - pot[0, at(before), :])
        qx = 0.5 * (pot[1, at(after), :] - pot[1, at(before), :])
        py, pz, qy, qz = yc(p), zc(p), yc(q), zc(q)
        disp_u[0, at(x), :] = px + d[0] * qx + d[5] * qy + d[4] * qz
        disp_u[1, at(x), :] = py + d[5] * qx + d[1] * qy + d[3] * qz
        disp_u[2, at(x), :] = pz + d[4] * qx + d[3] * qy + d[2] * qz

    def voxel(x, sums):
        after, before = lax.rem(x + 1, 32), lax.rem(x + 31, 32)
        ux, uy, uz = (disp_u[c, at(x), :] for c in range(3))
        dx = [0.5 * (disp_u[c, at(after), :] - disp_u[c, at(before), :]) for c in range(3)]
        gamma = [
            dx[0],
            yc(uy),
            zc(uz),
            0.5 * (yc(uz) + zc(uy)),
            0.5 * (dx[2] + zc(ux)),
            0.5 * (dx[1] + yc(ux)),
        ]
        flu[x] = jnp.concatenate([-g for g in gamma], axis=0).astype(wire)
        lame, shear = moduli(x)
        e = [load[c] - gamma[c] for c in range(6)]
        tr = e[0] + e[1] + e[2]
        dv = [e[c] - tr / 3.0 if c < 3 else e[c] for c in range(6)]
        scale, f = relaxed(shear, norm_of(dv), rates)
        twice = 2.0 * shear * scale
        bulk = (lame + (2.0 / 3.0) * shear) * tr
        new = [bulk + twice * dv[c] if c < 3 else twice * dv[c] for c in range(6)]
        new += [lame, shear / (1.0 + f)]
        return tuple(a + b for a, b in zip(sums, new))

    sums = lax.fori_loop(0, 32, voxel, tuple(jnp.zeros((8, 128), f32) for _ in range(8)))
    column = jnp.concatenate([jnp.sum(a, axis=0, keepdims=True) for a in sums], axis=0)
    column = jnp.sum(column, axis=1, keepdims=True) * (1.0 / VOX**3)
    lane8, row8 = lane_of((8, 128)), row_of((8, 128))
    own_row = jnp.sum(
        jnp.where(lane8 == row8 + group * 16, column, 0.0), axis=0, keepdims=True
    )
    for c in range(6):
        own_row = own_row + jnp.where(lane1 == group * 16 + 8 + c, load[c], 0.0)

    rowbuf[3] = own_row
    rows_out = []
    for i in range(1, 4):
        rows_out.append(
            pltpu.make_async_remote_copy(
                src_ref=rowbuf.at[3],
                dst_ref=rowbuf.at[i - 1],
                send_sem=y_send.at[i - 1],
                recv_sem=y_recv.at[i - 1],
                device_id={"grp": lax.rem(group + i, 4)},
                device_id_type=MESH,
            )
        )
        rows_out[-1].start()
    for copy in rows_out:
        copy.wait_recv()
    joined[0] = rowbuf[0] + rowbuf[1] + rowbuf[2] + rowbuf[3]
    everyone(lambda peer: joined.at[0], respbuf, resp_send, resp_recv)
    respbuf[me] = joined[0]
    everyone(lambda peer: flu.at[peer], flubuf, flu_send, flu_recv)
    flubuf[me] = flu[me]

    for k in range(3):
        for o in range(4):
            if k == 0 and o == 2:
                continue
            ref = (nb_disp, nb_force, nb_samp)[k].at[o]
            pltpu.make_async_copy(ref, ref, near_recv.at[k, o]).wait()
    exists = [(me * count + j >= 3).astype(f32) * (me * count + j < 67).astype(f32) for j in range(8)]

    def extended(own, near_ref, c):
        def get(ref, p):
            return ref[c, pl.ds(p, 1)] if c is not None else ref[pl.ds(p, 1)]

        planes = [get(near_ref.at[0], 1), get(near_ref.at[1], 0), get(near_ref.at[1], 1)]
        planes += [get(own, 0), get(own, 1)]
        planes += [get(near_ref.at[2], 0), get(near_ref.at[2], 1), get(near_ref.at[3], 0)]
        return planes

    def masked(planes):
        return jnp.concatenate([p * m for p, m in zip(planes, exists)], axis=0)

    around = [masked(extended(disp_ref, nb_disp, c)) for c in range(3)]
    outside = [masked(extended(force_ref, nb_force, c)) for c in range(3)]
    samples = extended(samp_ref, nb_samp, None)

    all_arrived(respbuf, resp_recv)
    gathered = jnp.concatenate([respbuf[r] for r in range(32)], axis=0)
    gathered = jnp.concatenate([gathered, jnp.zeros((96, 128), f32)], axis=0).T
    cells = []
    for c in range(8):
        row = jnp.concatenate(
            [gathered[g * 16 + c : g * 16 + c + 1, :32] for g in range(4)], axis=1
        )
        source = jnp.broadcast_to(row, (8, 128))
        cells.append(
            masked(
                [
                    jnp.take_along_axis(source, s[0], axis=1, mode="promise_in_bounds")[None]
                    for s in samples
                ]
            )
        )
    lame, shear = cells[6], cells[7]
    pull = force_of(cells[:6])
    res = [
        (outside[c][1:] - pull[c] - spring_rate * around[c][1:])
        * jnp.concatenate([jnp.full((1, 8, 128), m) for m in exists[1:]], axis=0)
        for c in range(3)
    ]

    def stiff(w, low):
        n = w[0].shape[0]
        strain = strain_of(w)
        stress = stress_of(strain, lame[low : low + n - 1], shear[low : low + n - 1])
        pull = force_of(stress)
        mask = jnp.concatenate(
            [jnp.full((1, 8, 128), m) for m in exists[low + 1 : low + n - 1]], axis=0
        )
        return [(pull[c] + spring_rate * w[c][1:-1]) * mask for c in range(3)]

    k1 = stiff(res, 1)
    k2 = stiff(k1, 2)
    r_own = [a[2:4] for a in res]
    k1_own = [a[1:3] for a in k1]
    k2_own = [a[0:2] for a in k2]
    energy_strain = strain_of(k2)
    energy_stress = stress_of(energy_strain, lame[3:5], shear[3:5])

    def dotted(a, b):
        total = a[0] * b[0]
        for c in range(1, 3):
            total = total + a[c] * b[c]
        return jnp.sum(jnp.sum(total, axis=0), axis=0, keepdims=True)

    energy = energy_strain[0] * energy_stress[0]
    for c in range(1, 6):
        energy = energy + (1.0 if c < 3 else 2.0) * energy_strain[c] * energy_stress[c]
    energy = jnp.sum(jnp.sum(energy, axis=0), axis=0, keepdims=True) + spring_rate * dotted(
        k2_own, k2_own
    )
    rows = [
        dotted(r_own, r_own),
        dotted(r_own, k1_own),
        dotted(k1_own, k1_own),
        dotted(k1_own, k2_own),
        dotted(k2_own, k2_own),
        energy,
        jnp.zeros((2, 128), f32),
    ]
    column = jnp.sum(jnp.concatenate(rows, axis=0), axis=1, keepdims=True)
    moment[0] = jnp.sum(jnp.where(lane8 == row8, column, 0.0), axis=0, keepdims=True)
    everyone(lambda peer: moment.at[0], momentbuf, mom_send, mom_recv)
    momentbuf[me] = moment[0]

    def owner(r, acc):
        taken = jnp.where(slot_ref[group * 32 + r] == me, 1.0, 0.0).astype(f32)
        return acc + taken * respbuf[r]

    row = lax.fori_loop(0, 32, owner, jnp.zeros((1, 128), f32))
    shifted = jnp.zeros((1, 128), f32)
    for g in range(4):
        here = (group == g).astype(f32)
        shifted = shifted + here * roll(row, -16 * g, 1)
    row_out[...] = jnp.broadcast_to(shifted, row_out.shape)

    table = jnp.concatenate([respbuf[r] for r in range(32)], axis=0)
    lane32 = lane_of((32, 128))
    group_load = [
        jnp.sum(jnp.where(lane32 == group * 16 + 8 + c, table, 0.0), axis=1, keepdims=True)
        for c in range(6)
    ]
    all_arrived(flubuf, flu_recv)
    for r in range(32):
        block = flubuf[r].astype(f32)
        for c in range(6):
            micro_out[pl.ds((c * 32 + r) * 8, 8), :] = (
                group_load[c][r : r + 1] + block[c * 8 : c * 8 + 8]
            )

    all_arrived(momentbuf, mom_recv)
    total = jnp.sum(momentbuf[...], axis=0)
    m = [pick(total, k) for k in range(6)]

    def form(a, b, first):
        out = 0.0
        for i, p in enumerate(a):
            for j, q in enumerate(b):
                out = out + p * q * m[i + j + first]
        return out

    rr = m[0]
    alpha0 = rr / m[1]
    r1 = (jnp.ones_like(rr), -alpha0)
    rr1 = form(r1, r1, 0)
    beta0 = rr1 / rr
    p1 = (1.0 + beta0, -alpha0)
    alpha1 = rr1 / form(p1, p1, 1)
    r2 = (jnp.ones_like(rr), -alpha0 - alpha1 * p1[0], alpha1 * alpha0)
    rr2 = form(r2, r2, 0)
    beta1 = rr2 / rr1
    p2 = (r2[0] + beta1 * p1[0], r2[1] + beta1 * p1[1], r2[2])
    alpha2 = rr2 / form(p2, p2, 1)
    weight = (
        alpha0 + alpha1 * p1[0] + alpha2 * p2[0],
        alpha1 * p1[1] + alpha2 * p2[1],
        alpha2 * p2[2],
    )
    for c in range(3):
        disp_out[c] = disp_ref[c] + (
            weight[0] * r_own[c] + weight[1] * k1_own[c] + weight[2] * k2_own[c]
        )

    for k in range(3):
        for copy in near[k]:
            copy.wait_send()
    for copy in rows_out:
        copy.wait_send()
    for buffer, sem in (
        (modbuf, mod_send), (partbuf, part_send), (respbuf, resp_send),
        (flubuf, flu_send), (momentbuf, mom_send),
    ):
        ref = buffer.at[pl.ds(0, 31)]
        pltpu.make_async_copy(ref, ref, sem).wait()


def shards(
    displacement, external_force, element_sample, lame_field, shear_field, plastic_steps, owner_slot
):
    count = displacement.shape[1]
    disp = displacement.reshape(3, count, 8, 128)
    force = external_force.reshape(3, count, 8, 128)
    sample = element_sample.reshape(count, 8, 128)
    moduli = jnp.concatenate(
        [lame_field.reshape(32, 8, 128), shear_field.reshape(32, 8, 128)], axis=1
    )
    constants = [jnp.asarray(t) for t in tables()]
    vmem = pl.BlockSpec(memory_space=pltpu.VMEM)
    smem = pl.BlockSpec(memory_space=pltpu.SMEM)
    dma = pltpu.SemaphoreType.DMA
    disp_next, row, micro = pl.pallas_call(
        kernel,
        out_shape=(
            jax.ShapeDtypeStruct(disp.shape, f32),
            jax.ShapeDtypeStruct((8, 128), f32),
            jax.ShapeDtypeStruct((6 * 32 * 8, 128), f32),
        ),
        in_specs=[smem] * 2 + [vmem] * 9,
        out_specs=(vmem,) * 3,
        scratch_shapes=[
            pltpu.VMEM((4,) + disp.shape, f32),
            pltpu.VMEM((4,) + disp.shape, f32),
            pltpu.VMEM((4,) + sample.shape, jnp.int32),
            pltpu.VMEM((32, 16, 128), bf16),
            pltpu.VMEM((32, 1, 128), f32),
            pltpu.VMEM((32, 1, 128), f32),
            pltpu.VMEM((count, 64, 128), f32),
            pltpu.VMEM((1024, 1024), bf16),
            pltpu.VMEM((1024, 1024), bf16),
            pltpu.VMEM((1024, 1024), bf16),
            pltpu.VMEM((1024, 1024), bf16),
            pltpu.VMEM((2, 256, 128), f32),
            pltpu.VMEM((2, 256, 128), f32),
            pltpu.VMEM((3, 256, 128), f32),
            pltpu.VMEM((32, 48, 128), wire),
            pltpu.VMEM((32, 48, 128), wire),
            pltpu.VMEM((4, 1, 128), f32),
            pltpu.VMEM((1, 1, 128), f32),
            pltpu.VMEM((32, 1, 128), f32),
            pltpu.VMEM((1, 1, 128), f32),
            pltpu.VMEM((32, 1, 128), f32),
            dma((3, 4)), dma((3, 4)), dma, dma, dma, dma,
            dma((3,)), dma((3,)), dma, dma, dma, dma, dma, dma,
        ],
        compiler_params=pltpu.CompilerParams(collective_id=0, has_side_effects=True),
    )(plastic_steps, owner_slot, disp, force, sample, moduli, *constants)
    return (
        disp_next.reshape(displacement.shape),
        row[:1, :8],
        micro.reshape(6, 32, 1, 1024),
    )


def solution(mesh):
    in_specs = (
        P(None, "dev", None, None),
        P(None, "dev", None, None),
        P("dev", None, None),
        P("grp", "dev", None),
        P("grp", "dev", None),
        P(),
        P(),
    )
    out_specs = (P(None, "dev", None, None), P(("grp", "dev"), None), P(None, "grp", "dev", None))
    return jax.shard_map(shards, mesh=mesh, in_specs=in_specs, out_specs=out_specs, check_vma=False)
```

profile of v0, /device:TPU:1, one launch (start us, length us, event | category | flops | bytes accessed | tf_op | source)
XLA Modules:
  0.0 57.4 jit_solution(1472150372988405045)
XLA Ops:
  0.6 0.0 copy-start.2
  0.6 0.9 %copy.17 = bf16[4,8,8,128]{3,2,1,0:T(8,128)(2,1)S(1)} copy(bf16[4,8,8,128]{3,1,2,0:T(8,128)(2,1)} %bitcast.18) | data formatting | bytes 131072
  1.5 0.0 copy-done.2
  1.6 0.0 copy-start
  1.6 0.7 %pad_maximum_fusion.mod_ref = bf16[32,16,128]{2,1,0:T(8,128)(2,1)} fusion(bf16[32,8,128]{2,1,0:T(8,128)(2,1)S(1)} %bitcast.16, bf16[32,8,128]{2,1,0:T(8,128)(2,1)S(1)} %bitcast.17), kind=kLoop, calls=%fused_computation | loop fusion | flops 262144 | bytes 262144 | tf_op jit(solution)/shard_map/concatenate | solution.py:640
  2.2 0.2 copy-done
  2.5 0.0 copy-start.1
  2.5 0.7 %reshape.27.disp_ref = f32[3,2,8,128]{3,2,1,0:T(8,128)} reshape(f32[3,2,32,32]{3,2,1,0:T(8,128)S(1)} %copy-done) | data formatting | bytes 49152 | tf_op jit(solution)/shard_map/reshape | solution.py:637
  3.1 0.2 copy-done.1
  3.3 0.0 copy-start.3
  3.3 0.7 %reshape.28.force_ref = f32[3,2,8,128]{3,2,1,0:T(8,128)} reshape(f32[3,2,32,32]{3,2,1,0:T(8,128)S(1)} %copy-done.1) | data formatting | bytes 49152 | tf_op jit(solution)/shard_map/reshape | solution.py:638
  4.0 0.1 copy-done.3
  4.1 0.7 %reshape.29.samp_ref = s32[2,8,128]{2,1,0:T(8,128)} reshape(s32[2,32,32]{2,1,0:T(8,128)S(1)} %copy-done.3) | data formatting | bytes 16384 | tf_op jit(solution)/shard_map/reshape | solution.py:639
  4.8 47.4 %shard_map.139 = (f32[3,2,8,128]{3,2,1,0:T(8,128)}, f32[8,128]{1,0:T(8,128)}, f32[1536,128]{1,0:T(8,128)}) custom-call(s32[128]{0:T(128)} %steps_ref.1, s32[128]{0:T(128)} %slot_ref.1, f32[3,2,8,128]{3,2,1,0:T(8,128)} %reshape.27.disp_ref, f32[3,2,8,128]{3,2,1,0:T(8,128)} %reshape.28.force_ref, s32[2,8,128]{2,1,0:T(8,128)} %reshape.29.samp_ref, ...), custom_call_target="tpu_custom_call" | custom-call | tf_op jit(solution)/shard_map/pallas_call | solution.py:647
  52.2 1.5 %reshape.32 = f32[3,2,32,32]{3,2,1,0:T(8,128)} reshape(f32[3,2,8,128]{3,2,1,0:T(8,128)} %get-tuple-element.6) | data formatting | bytes 49152 | tf_op jit(solution)/shard_map/reshape | solution.py:684
  53.6 1.2 %slice.3 = f32[1,8]{1,0:T(1,128)} slice(f32[8,128]{1,0:T(8,128)} %get-tuple-element.7), slice={[0:1], [0:8]} | slice | bytes 64 | tf_op jit(solution)/shard_map/slice | solution.py:685
  54.8 2.6 %copy.19 = f32[6,32,1,1024]{3,2,1,0:T(1,128)} copy(f32[6,32,1,1024]{3,2,1,0:T(1,128)} %bitcast.15) | data formatting | bytes 1572864
  (1 shorter events, 0.0 us)
Async XLA Ops:
  0.6 0.9 %copy-start.2 = (bf16[32,1,1024]{2,0,1:T(8,128)(2,1)S(1)}, bf16[32,1,1024]{2,0,1:T(8,128)(2,1)}, u32[]{:S(2)}) copy-start(bf16[32,1,1024]{2,0,1:T(8,128)(2,1)} %param.15) | copy-start | bytes 196612
  1.6 0.9 %copy-start = (f32[3,2,32,32]{3,2,1,0:T(8,128)S(1)}, f32[3,2,32,32]{3,2,1,0:T(8,128)}, u32[]{:S(2)}) copy-start(f32[3,2,32,32]{3,2,1,0:T(8,128)} %param.12) | copy-start | bytes 73732
  2.5 0.9 %copy-start.1 = (f32[3,2,32,32]{3,2,1,0:T(8,128)S(1)}, f32[3,2,32,32]{3,2,1,0:T(8,128)}, u32[]{:S(2)}) copy-start(f32[3,2,32,32]{3,2,1,0:T(8,128)} %param.13) | copy-start | bytes 73732
  3.3 0.8 %copy-start.3 = (s32[2,32,32]{2,1,0:T(8,128)S(1)}, s32[2,32,32]{2,1,0:T(8,128)}, u32[]{:S(2)}) copy-start(s32[2,32,32]{2,1,0:T(8,128)} %param.14) | copy-start | bytes 24580
where the time goes:
time: 57.8 us; the launch traced here: 57.4 us
  Pallas kernels  47.4 us (82%)
  local copies, waits for them, and re-layouts  8.62 us (15%)
  other arithmetic  0.68 us (1%)
  between operations  0.68 us (1%)
    pallas_call x1, Pallas kernels, shards(): pl.pallas_call(kernel, out_shape=(jax.ShapeDtypeStruct(disp.shape, f32),...  47.4 us
    unnamed x11, local copies, waits for them, and re-layouts  3.92 us
    reshape x1, local copies, waits for them, and re-layouts, shards(): disp_next.reshape(displacement.shape)  1.46 us
    slice x1, local copies, waits for them, and re-layouts, shards(): row[:1, :8]  1.18 us

commit v1 on v0

--- a/solution.py
+++ b/solution.py
@@ -182,9 +182,11 @@
 
 
 def kernel(
-    steps_ref, slot_ref, disp_ref, force_ref, samp_ref, mod_ref,
-    wt_ref, vt_ref, vz_ref, x_ref, spec_ref,
+    disp_in, wt_in, lame_in, shear_in, force_in, samp_in, vt_in, vz_in, x_in, spec_in, steps_in, slot_in,
     disp_out, row_out, micro_out,
+    disp_raw, wt_ref, lame_raw, shear_raw, force_raw, samp_raw, vt_ref, vz_ref, x_ref, spec_ref,
+    steps_ref, slot_ref, in_sem,
+    disp_ref, force_ref, samp_ref, mod_ref, modwide,
     nb_disp, nb_force, nb_samp, modbuf, part, partbuf, strainrow,
     wh, wl, vh, vl, field, pot, disp_u, flu, flubuf,
     rowbuf, joined, respbuf, moment, momentbuf,
@@ -193,10 +195,23 @@
 ):
     me = lax.axis_index("dev")
     group = lax.axis_index("grp")
-    count = disp_ref.shape[1]
+    count = disp_raw.shape[1]
 
     def peer_of(i):
         return lax.rem(me + i, 32)
+
+    loads = [
+        pltpu.make_async_copy(source, target, in_sem.at[k])
+        for k, (source, target) in enumerate(
+            (
+                (disp_in, disp_raw), (wt_in, wt_ref), (lame_in, lame_raw), (shear_in, shear_raw),
+                (force_in, force_raw), (samp_in, samp_raw), (vt_in, vt_ref), (vz_in, vz_ref),
+                (x_in, x_ref), (spec_in, spec_ref), (steps_in, steps_ref), (slot_in, slot_ref),
+            )
+        )
+    ]
+    for copy in loads:
+        copy.start()
 
     barrier = pltpu.get_barrier_semaphore()
 
@@ -209,6 +224,21 @@
             barrier, inc=1, device_id={"grp": lax.rem(group + i, 4)}, device_id_type=MESH
         )
 
+    for k in (0, 2, 3, 4, 5):
+        loads[k].wait()
+    for raw, dense in ((disp_raw, disp_ref), (force_raw, force_ref), (samp_raw, samp_ref)):
+        for index in np.ndindex(raw.shape[:-2]):
+            dense[index] = jnp.concatenate(
+                [raw[(*index, pl.ds(q, 8, stride=4), slice(None))] for q in range(4)], axis=1
+            )
+    for k, raw in enumerate((lame_raw, shear_raw)):
+        wide = raw[...].astype(f32)
+        for t in range(8):
+            modwide[pl.ds(k * 8 + t, 32, stride=16), :] = wide[:, t * 128 : t * 128 + 128]
+    for r in range(32):
+        mod_ref[r] = modwide[pl.ds(r * 16, 16), :].astype(bf16)
+
+    loads[1].wait()
     part[...] = jnp.zeros_like(part)
 
     @pl.loop(0, 32)
@@ -307,6 +337,8 @@
         part[r, :, pl.ds(0, 8)] = sums[r : r + 1]
     everyone(lambda peer: part.at[peer], partbuf, part_send, part_recv)
     partbuf[me] = part[me]
+    for k in range(6, 12):
+        loads[k].wait()
 
     @pl.loop(0, 32)
     def _(k):
@@ -568,7 +600,7 @@
     for g in range(4):
         here = (group == g).astype(f32)
         shifted = shifted + here * roll(row, -16 * g, 1)
-    row_out[...] = jnp.broadcast_to(shifted, row_out.shape)
+    row_out[...] = shifted[:, :8]
 
     table = jnp.concatenate([respbuf[r] for r in range(32)], axis=0)
     lane32 = lane_of((32, 128))
@@ -613,9 +645,12 @@
         alpha2 * p2[2],
     )
     for c in range(3):
-        disp_out[c] = disp_ref[c] + (
+        new = disp_ref[c] + (
             weight[0] * r_own[c] + weight[1] * k1_own[c] + weight[2] * k2_own[c]
         )
+        for p in range(count):
+            for q in range(4):
+                disp_out[c, p, pl.ds(q, 8, stride=4), :] = new[p][:, q * 32 : q * 32 + 32]
 
     for k in range(3):
         for copy in near[k]:
@@ -634,29 +669,45 @@
     displacement, external_force, element_sample, lame_field, shear_field, plastic_steps, owner_slot
 ):
     count = displacement.shape[1]
-    disp = displacement.reshape(3, count, 8, 128)
-    force = external_force.reshape(3, count, 8, 128)
-    sample = element_sample.reshape(count, 8, 128)
-    moduli = jnp.concatenate(
-        [lame_field.reshape(32, 8, 128), shear_field.reshape(32, 8, 128)], axis=1
-    )
-    constants = [jnp.asarray(t) for t in tables()]
+    disp, sample = (3, count, 8, 128), (count, 8, 128)
+    wt, vt, vz, x, spec = (jnp.asarray(t) for t in tables())
+    operands = (
+        displacement,
+        wt,
+        lame_field.reshape(32, 1024),
+        shear_field.reshape(32, 1024),
+        external_force,
+        element_sample,
+        vt,
+        vz,
+        x,
+        spec,
+    )
+    scalars = (plastic_steps, owner_slot)
     vmem = pl.BlockSpec(memory_space=pltpu.VMEM)
-    smem = pl.BlockSpec(memory_space=pltpu.SMEM)
+    hbm = pl.BlockSpec(memory_space=pltpu.HBM)
     dma = pltpu.SemaphoreType.DMA
     disp_next, row, micro = pl.pallas_call(
         kernel,
         out_shape=(
-            jax.ShapeDtypeStruct(disp.shape, f32),
-            jax.ShapeDtypeStruct((8, 128), f32),
+            jax.ShapeDtypeStruct(displacement.shape, f32),
+            jax.ShapeDtypeStruct((1, 8), f32),
             jax.ShapeDtypeStruct((6 * 32 * 8, 128), f32),
         ),
-        in_specs=[smem] * 2 + [vmem] * 9,
+        in_specs=[hbm] * 12,
         out_specs=(vmem,) * 3,
         scratch_shapes=[
-            pltpu.VMEM((4,) + disp.shape, f32),
-            pltpu.VMEM((4,) + disp.shape, f32),
-            pltpu.VMEM((4,) + sample.shape, jnp.int32),
+            *(pltpu.VMEM(a.shape, a.dtype) for a in operands),
+            *(pltpu.SMEM(a.shape, a.dtype) for a in scalars),
+            dma((12,)),
+            pltpu.VMEM(disp, f32),
+            pltpu.VMEM(disp, f32),
+            pltpu.VMEM(sample, jnp.int32),
+            pltpu.VMEM((32, 16, 128), bf16),
+            pltpu.VMEM((512, 128), f32),
+            pltpu.VMEM((4,) + disp, f32),
+            pltpu.VMEM((4,) + disp, f32),
+            pltpu.VMEM((4,) + sample, jnp.int32),
             pltpu.VMEM((32, 16, 128), bf16),
             pltpu.VMEM((32, 1, 128), f32),
             pltpu.VMEM((32, 1, 128), f32),
@@ -678,13 +729,9 @@
             dma((3, 4)), dma((3, 4)), dma, dma, dma, dma,
             dma((3,)), dma((3,)), dma, dma, dma, dma, dma, dma,
         ],
-        compiler_params=pltpu.CompilerParams(collective_id=0, has_side_effects=True),
-    )(plastic_steps, owner_slot, disp, force, sample, moduli, *constants)
-    return (
-        disp_next.reshape(displacement.shape),
-        row[:1, :8],
-        micro.reshape(6, 32, 1, 1024),
-    )
+        compiler_params=pltpu.CompilerParams(collective_id=0, has_side_effects=True, vmem_limit_bytes=24 << 20),
+    )(*[pltpu.with_memory_space_constraint(a, pltpu.HBM) for a in operands + scalars])
+    return disp_next, row, micro.reshape(6, 32, 1, 1024)
 
 
 def solution(mesh):

time: 57.8 us -> 48.2 us (0.83)
  local copies, waits for them, and re-layouts: 8.62 us -> 2.03 us
  Pallas kernels: 47.4 us -> 45.4 us
  other arithmetic: 0.68 us -> 0 us
    reshape x4 -> x0, local copies, waits for them, and re-layouts: 3.52 us -> none  [the longest x1 1.46 us: shards(): disp_next.reshape(displacement.shape)]
    pallas_call x1, Pallas kernels: 47.4 us -> 45.4 us  [shards(): pl.pallas_call(kernel, out_shape=(jax.ShapeDtypeStruct(displacement.shape...]
    unnamed x11 -> x3, local copies, waits for them, and re-layouts: 3.92 us -> 2.03 us
    slice x1 -> x0, local copies, waits for them, and re-layouts: 1.18 us -> none  [shards(): row[:1, :8]]
    concatenate x1 -> x0, other arithmetic: 0.68 us -> none  [shards(): jnp.concatenate([lame_field.reshape(32, 8, 128), shear_field.reshape(32,...]
where the time goes in v1:
time: 48.2 us; the launch traced here: 48.1 us
  Pallas kernels  45.4 us (94%)
  local copies, waits for them, and re-layouts  2.03 us (4%)
  between operations  0.64 us (1%)
    pallas_call x1, Pallas kernels, shards(): pl.pallas_call(kernel, out_shape=(jax.ShapeDtypeStruct(displacement.shape...  45.4 us
    unnamed x3, local copies, waits for them, and re-layouts  2.03 us

profile of v1, /device:TPU:1, one launch (start us, length us, event | category | flops | bytes accessed | tf_op | source)
XLA Modules:
  0.0 48.1 jit_solution(18169960896293970007)
XLA Ops:
  0.6 45.4 %shard_map.139 = (f32[3,2,32,32]{3,2,1,0:T(8,128)S(1)}, f32[1,8]{1,0:T(1,128)S(1)}, f32[1536,128]{1,0:T(8,128)S(1)}) custom-call(f32[3,2,32,32]{3,2,1,0:T(8,128)} %disp_in.1, f32[4,32,512]{2,1,0:T(8,128)} %constant.10.clone.wt_in, bf16[32,1024]{1,0:T(8,128)(2,1)} %bitcast.4, bf16[32,1024]{1,0:T(8,128)(2,1)} %bitcast.5, f32[3,2,32,32]{3,2,1,0:T(8,128)} %force_in.1, ...), custom_call_target="tpu_custom_call" | custom-call | tf_op jit(solution)/shard_map/pallas_call | solution.py:690
  46.0 0.6 %copy.19 = f32[3,2,32,32]{3,2,1,0:T(8,128)} copy(f32[3,2,32,32]{3,2,1,0:T(8,128)S(1)} %get-tuple-element.15) | data formatting | bytes 49152
  46.7 0.5 %copy.20 = f32[1,8]{1,0:T(1,128)} copy(f32[1,8]{1,0:T(1,128)S(1)} %get-tuple-element.16) | data formatting | bytes 64
  47.2 0.9 %copy.21 = f32[6,32,1,1024]{3,2,1,0:T(1,128)} copy(f32[6,32,1,1024]{3,2,1,0:T(1,128)S(1)} %bitcast.3) | data formatting | bytes 1572864

commit v2 on v1

--- a/solution.py
+++ b/solution.py
@@ -115,18 +115,28 @@
 
 def zc(v):
     lane = lane_of(v.shape) % VOX
-    up = jnp.where(lane == VOX - 1, roll(v, 31, 1), roll(v, -1, 1))
-    down = jnp.where(lane == 0, roll(v, -31, 1), roll(v, 1, 1))
+    up = jnp.where(lane == VOX - 1, roll(v, 31, 2), roll(v, -1, 2))
+    down = jnp.where(lane == 0, roll(v, -31, 2), roll(v, 1, 2))
     return 0.5 * (up - down)
 
 
 def yc(v):
     lane = lane_of(v.shape)
-    up = roll(v, -VOX, 1)
-    up = jnp.where(lane < 96, up, roll(up, -1, 0))
-    down = roll(v, VOX, 1)
-    down = jnp.where(lane >= VOX, down, roll(down, 1, 0))
+    up = roll(v, -VOX, 2)
+    up = jnp.where(lane < 96, up, roll(up, -1, 1))
+    down = roll(v, VOX, 2)
+    down = jnp.where(lane >= VOX, down, roll(down, 1, 1))
     return 0.5 * (up - down)
+
+
+def spans(distance):
+    return min(distance, 4 - distance)
+
+
+OTHERS = sorted(
+    ((a, b, c) for a in range(4) for b in range(4) for c in range(2) if (a, b, c) != (0, 0, 0)),
+    key=lambda p: (-spans(p[0]) - spans(p[1]), -p[2], p),
+)
 
 
 def strain_of(fields):
@@ -187,18 +197,21 @@
     disp_raw, wt_ref, lame_raw, shear_raw, force_raw, samp_raw, vt_ref, vz_ref, x_ref, spec_ref,
     steps_ref, slot_ref, in_sem,
     disp_ref, force_ref, samp_ref, mod_ref, modwide,
-    nb_disp, nb_force, nb_samp, modbuf, part, partbuf, strainrow,
-    wh, wl, vh, vl, field, pot, disp_u, flu, flubuf,
+    nb_first, nb_disp, nb_force, nb_samp, modbuf, part, partbuf, strainrow,
+    wh, wl, vh, vl, field, pot, disp_u, gam, flu, flubuf,
     rowbuf, joined, respbuf, moment, momentbuf,
-    near_send, near_recv, mod_send, mod_recv, part_send, part_recv,
+    first_sem, near_send, near_recv, mod_send, mod_recv, part_send, part_recv,
     y_send, y_recv, resp_send, resp_recv, flu_send, flu_recv, mom_send, mom_recv,
 ):
     me = lax.axis_index("dev")
     group = lax.axis_index("grp")
     count = disp_raw.shape[1]
 
-    def peer_of(i):
-        return lax.rem(me + i, 32)
+    me_x, me_z, me_c = me // 8, lax.rem(me // 2, 4), lax.rem(me, 2)
+    at_x = [lax.rem(me_x + k, 4) * 8 for k in range(4)]
+    at_z = [lax.rem(me_z + k, 4) * 2 for k in range(4)]
+    at_c = [me_c, 1 - me_c]
+    peers = [at_x[a] + at_z[b] + at_c[c] for a, b, c in OTHERS]
 
     loads = [
         pltpu.make_async_copy(source, target, in_sem.at[k])
@@ -215,10 +228,8 @@
 
     barrier = pltpu.get_barrier_semaphore()
 
-    @pl.loop(1, 32)
-    def _(i):
-        pl.semaphore_signal(barrier, inc=1, device_id={"dev": peer_of(i)}, device_id_type=MESH)
-
+    for peer in peers:
+        pl.semaphore_signal(barrier, inc=1, device_id={"dev": peer}, device_id_type=MESH)
     for i in range(1, 4):
         pl.semaphore_signal(
             barrier, inc=1, device_id={"grp": lax.rem(group + i, 4)}, device_id_type=MESH
@@ -238,19 +249,7 @@
     for r in range(32):
         mod_ref[r] = modwide[pl.ds(r * 16, 16), :].astype(bf16)
 
-    loads[1].wait()
     part[...] = jnp.zeros_like(part)
-
-    @pl.loop(0, 32)
-    def _(y):
-        c, s = wt_ref[0, pl.ds(y, 1), :], wt_ref[1, pl.ds(y, 1), :]
-        zr, zi = wt_ref[2], wt_ref[3]
-        rows = pl.ds(pl.multiple_of(y * 32, 32), 32)
-        for k, block in enumerate((c * zr + s * zi, c * zi - s * zr)):
-            high, low = split(block)
-            wh[rows, pl.ds(k * HALF, HALF)] = high
-            wl[rows, pl.ds(k * HALF, HALF)] = low
-
     pl.semaphore_wait(barrier, 34)
 
     def near_copies(source, target, k):
@@ -273,13 +272,18 @@
         near_copies(force_ref, nb_force, 1),
         near_copies(samp_ref, nb_samp, 2),
     ]
-    for o in (1, 2, 3, 0):
-        near[0][o].start()
+    first_plane = pltpu.make_async_remote_copy(
+        src_ref=disp_ref.at[:, 0],
+        dst_ref=nb_first,
+        send_sem=first_sem.at[0],
+        recv_sem=first_sem.at[1],
+        device_id={"dev": lax.rem(me + 31, 32)},
+        device_id_type=MESH,
+    )
+    first_plane.start()
 
     def everyone(source, target, send, recv):
-        @pl.loop(1, 32)
-        def _(i):
-            peer = peer_of(i)
+        for peer in peers:
             pltpu.make_async_remote_copy(
                 src_ref=source(peer),
                 dst_ref=target.at[me],
@@ -294,15 +298,24 @@
         pltpu.make_async_copy(ref, ref, recv).wait()
 
     everyone(lambda peer: mod_ref.at[peer], modbuf, mod_send, mod_recv)
-    for k in (1, 2):
-        for copy in near[k]:
-            copy.start()
     modbuf[me] = mod_ref[me]
 
-    pltpu.make_async_copy(disp_ref, nb_disp.at[2], near_recv.at[0, 2]).wait()
+    loads[1].wait()
+
+    @pl.loop(0, 32)
+    def _(y):
+        c, s = wt_ref[0, pl.ds(y, 1), :], wt_ref[1, pl.ds(y, 1), :]
+        zr, zi = wt_ref[2], wt_ref[3]
+        rows = pl.ds(pl.multiple_of(y * 32, 32), 32)
+        for k, block in enumerate((c * zr + s * zi, c * zi - s * zr)):
+            high, low = split(block)
+            wh[rows, pl.ds(k * HALF, HALF)] = high
+            wl[rows, pl.ds(k * HALF, HALF)] = low
+
+    first_plane.wait_recv()
     inside_up = (me < 31).astype(f32)
     fields = [
-        jnp.concatenate([disp_ref[c], nb_disp[2, c][:1] * inside_up], axis=0) for c in range(3)
+        jnp.concatenate([disp_ref[c], nb_first[pl.ds(c, 1)] * inside_up], axis=0) for c in range(3)
     ]
     strain = strain_of(fields)
     one_hots, rows_high, rows_low = [], [], []
@@ -337,6 +350,9 @@
         part[r, :, pl.ds(0, 8)] = sums[r : r + 1]
     everyone(lambda peer: part.at[peer], partbuf, part_send, part_recv)
     partbuf[me] = part[me]
+    for k in range(3):
+        for copy in near[k]:
+            copy.start()
     for k in range(6, 12):
         loads[k].wait()
 
@@ -353,9 +369,22 @@
     ref = modbuf.at[pl.ds(0, 31)]
     pltpu.make_async_copy(ref, ref, mod_recv).wait()
 
-    def moduli(x):
-        both = modbuf[x].astype(f32)
-        return both[:8], both[8:]
+    def moduli(x, n):
+        both = modbuf[pl.ds(x, n)].astype(f32)
+        return both[:, :8], both[:, 8:]
+
+    def at(x, n):
+        return pl.ds(pl.multiple_of(x * 8, 8), n * 8)
+
+    def planes(ref, k, x, n):
+        return ref[k, at(x, n), :].reshape(n, 8, 128)
+
+    def x_slope(ref, k, x, n, v):
+        after = planes(ref, k, lax.rem(x + n, 32), 1)
+        before = planes(ref, k, lax.rem(x + 31, 32), 1)
+        up = jnp.concatenate([v[1:], after], axis=0)
+        down = jnp.concatenate([before, v[:-1]], axis=0)
+        return 0.5 * (up - down)
 
     def forward(slot):
         rows = jnp.concatenate(
@@ -366,10 +395,10 @@
         plane = both[:32] + (both[32:] + mm(high, wl[...]))
         return product(x_ref[0], jnp.concatenate([plane[:, :HALF], plane[:, HALF:]], axis=0))
 
-    @pl.loop(0, 32)
-    def _(x):
-        lame, shear = moduli(x)
-        field[0, pl.ds(pl.multiple_of(x * 8, 8), 8), :] = lame + (2.0 / 3.0) * shear
+    @pl.loop(0, 4)
+    def _(t):
+        lame, shear = moduli(t * 8, 8)
+        field[0, at(t * 8, 8), :] = (lame + (2.0 / 3.0) * shear).reshape(64, 128)
 
     spectrum_a = forward(0)
 
@@ -389,11 +418,11 @@
     rates = [jnp.where(k < own_steps, relax_rate, 0.0).astype(f32) for k in range(KMAX)]
     size = norm_of(d)
 
-    @pl.loop(0, 32)
-    def _(x):
-        _, shear = moduli(x)
+    @pl.loop(0, 4)
+    def _(t):
+        _, shear = moduli(t * 8, 8)
         scale, _ = relaxed(shear, size, rates)
-        field[1, pl.ds(pl.multiple_of(x * 8, 8), 8), :] = 2.0 * shear * scale
+        field[1, at(t * 8, 8), :] = (2.0 * shear * scale).reshape(64, 128)
 
     spectrum_b = forward(1)
     mix = d[0] * spec_ref[1]
@@ -428,35 +457,63 @@
         for s in range(8):
             pot[k, pl.ds(s, 32, stride=8), :] = space[k * 32 : k * 32 + 32, s * 128 : s * 128 + 128]
 
-    def at(x):
-        return pl.ds(pl.multiple_of(x * 8, 8), 8)
-
-    @pl.loop(0, 32)
-    def _(x):
-        after, before = lax.rem(x + 1, 32), lax.rem(x + 31, 32)
-        p, q = pot[0, at(x), :], pot[1, at(x), :]
-        px = 0.5 * (pot[0, at(after), :] - pot[0, at(before), :])
-        qx = 0.5 * (pot[1, at(after), :] - pot[1, at(before), :])
+    @pl.loop(0, 8)
+    def _(t):
+        x = t * 4
+        p, q = planes(pot, 0, x, 4), planes(pot, 1, x, 4)
+        px, qx = x_slope(pot, 0, x, 4, p), x_slope(pot, 1, x, 4, q)
         py, pz, qy, qz = yc(p), zc(p), yc(q), zc(q)
-        disp_u[0, at(x), :] = px + d[0] * qx + d[5] * qy + d[4] * qz
-        disp_u[1, at(x), :] = py + d[5] * qx + d[1] * qy + d[3] * qz
-        disp_u[2, at(x), :] = pz + d[4] * qx + d[3] * qy + d[2] * qz
-
-    def voxel(x, sums):
-        after, before = lax.rem(x + 1, 32), lax.rem(x + 31, 32)
-        ux, uy, uz = (disp_u[c, at(x), :] for c in range(3))
-        dx = [0.5 * (disp_u[c, at(after), :] - disp_u[c, at(before), :]) for c in range(3)]
-        gamma = [
-            dx[0],
-            yc(uy),
-            zc(uz),
-            0.5 * (yc(uz) + zc(uy)),
-            0.5 * (dx[2] + zc(ux)),
-            0.5 * (dx[1] + yc(ux)),
+        ux = px + d[0] * qx + d[5] * qy + d[4] * qz
+        uy = py + d[5] * qx + d[1] * qy + d[3] * qz
+        uz = pz + d[4] * qx + d[3] * qy + d[2] * qz
+        for c, u in enumerate((ux, uy, uz)):
+            disp_u[c, at(x, 4), :] = u.reshape(32, 128)
+
+    def send_planes(t):
+        for b, c in sorted(((b, c) for b in range(4) for c in range(2)), key=lambda p: -spans(p[0])):
+            peer = lax.rem(me_x + 2 + t, 4) * 8 + at_z[b] + at_c[c]
+
+            def start(peer=peer):
+                pltpu.make_async_remote_copy(
+                    src_ref=flu.at[peer],
+                    dst_ref=flubuf.at[me],
+                    send_sem=flu_send,
+                    recv_sem=flu_recv,
+                    device_id={"dev": peer},
+                    device_id_type=MESH,
+                ).start()
+
+            if (b, c) == (0, 0):
+                pl.when(t != 2)(start)
+            else:
+                start()
+
+    @pl.loop(0, 4)
+    def _(t):
+        x = lax.rem(me_x + 2 + t, 4) * 8
+        ux, uy, uz = (planes(disp_u, c, x, 8) for c in range(3))
+        dx = [x_slope(disp_u, c, x, 8, u) for c, u in enumerate((ux, uy, uz))]
+        change = [
+            -dx[0],
+            -yc(uy),
+            -zc(uz),
+            -0.5 * (yc(uz) + zc(uy)),
+            -0.5 * (dx[2] + zc(ux)),
+            -0.5 * (dx[1] + yc(ux)),
         ]
-        flu[x] = jnp.concatenate([-g for g in gamma], axis=0).astype(wire)
-        lame, shear = moduli(x)
-        e = [load[c] - gamma[c] for c in range(6)]
+        for c in range(6):
+            gam[c, at(x, 8), :] = change[c].reshape(64, 128)
+        for k in range(3):
+            pair = jnp.concatenate(change[2 * k : 2 * k + 2], axis=1)
+            flu[pl.ds(x, 8), pl.ds(k * 16, 16), :] = pair.astype(wire)
+        send_planes(t)
+
+    flubuf[me] = flu[me]
+
+    def voxel(t, sums):
+        x = t * 4
+        lame, shear = moduli(x, 4)
+        e = [load[c] + planes(gam, c, x, 4) for c in range(6)]
         tr = e[0] + e[1] + e[2]
         dv = [e[c] - tr / 3.0 if c < 3 else e[c] for c in range(6)]
         scale, f = relaxed(shear, norm_of(dv), rates)
@@ -464,9 +521,9 @@
         bulk = (lame + (2.0 / 3.0) * shear) * tr
         new = [bulk + twice * dv[c] if c < 3 else twice * dv[c] for c in range(6)]
         new += [lame, shear / (1.0 + f)]
-        return tuple(a + b for a, b in zip(sums, new))
-
-    sums = lax.fori_loop(0, 32, voxel, tuple(jnp.zeros((8, 128), f32) for _ in range(8)))
+        return tuple(a + jnp.sum(b, axis=0) for a, b in zip(sums, new))
+
+    sums = lax.fori_loop(0, 8, voxel, tuple(jnp.zeros((8, 128), f32) for _ in range(8)))
     column = jnp.concatenate([jnp.sum(a, axis=0, keepdims=True) for a in sums], axis=0)
     column = jnp.sum(column, axis=1, keepdims=True) * (1.0 / VOX**3)
     lane8, row8 = lane_of((8, 128)), row_of((8, 128))
@@ -495,13 +552,9 @@
     joined[0] = rowbuf[0] + rowbuf[1] + rowbuf[2] + rowbuf[3]
     everyone(lambda peer: joined.at[0], respbuf, resp_send, resp_recv)
     respbuf[me] = joined[0]
-    everyone(lambda peer: flu.at[peer], flubuf, flu_send, flu_recv)
-    flubuf[me] = flu[me]
 
     for k in range(3):
         for o in range(4):
-            if k == 0 and o == 2:
-                continue
             ref = (nb_disp, nb_force, nb_samp)[k].at[o]
             pltpu.make_async_copy(ref, ref, near_recv.at[k, o]).wait()
     exists = [(me * count + j >= 3).astype(f32) * (me * count + j < 67).astype(f32) for j in range(8)]
@@ -652,6 +705,7 @@
             for q in range(4):
                 disp_out[c, p, pl.ds(q, 8, stride=4), :] = new[p][:, q * 32 : q * 32 + 32]
 
+    first_plane.wait_send()
     for k in range(3):
         for copy in near[k]:
             copy.wait_send()
@@ -663,6 +717,17 @@
     ):
         ref = buffer.at[pl.ds(0, 31)]
         pltpu.make_async_copy(ref, ref, sem).wait()
+
+
+def leave(a, b, c, a_out, b_out, c_out, sem):
+    copies = [
+        pltpu.make_async_copy(source, target, sem.at[k])
+        for k, (source, target) in enumerate(((c, c_out), (a, a_out), (b, b_out)))
+    ]
+    for copy in copies:
+        copy.start()
+    for copy in copies:
+        copy.wait()
 
 
 def shards(
@@ -705,6 +770,7 @@
             pltpu.VMEM(sample, jnp.int32),
             pltpu.VMEM((32, 16, 128), bf16),
             pltpu.VMEM((512, 128), f32),
+            pltpu.VMEM((3, 8, 128), f32),
             pltpu.VMEM((4,) + disp, f32),
             pltpu.VMEM((4,) + disp, f32),
             pltpu.VMEM((4,) + sample, jnp.int32),
@@ -719,6 +785,7 @@
             pltpu.VMEM((2, 256, 128), f32),
             pltpu.VMEM((2, 256, 128), f32),
             pltpu.VMEM((3, 256, 128), f32),
+            pltpu.VMEM((6, 256, 128), f32),
             pltpu.VMEM((32, 48, 128), wire),
             pltpu.VMEM((32, 48, 128), wire),
             pltpu.VMEM((4, 1, 128), f32),
@@ -726,11 +793,20 @@
             pltpu.VMEM((32, 1, 128), f32),
             pltpu.VMEM((1, 1, 128), f32),
             pltpu.VMEM((32, 1, 128), f32),
-            dma((3, 4)), dma((3, 4)), dma, dma, dma, dma,
+            dma((2,)), dma((3, 4)), dma((3, 4)), dma, dma, dma, dma,
             dma((3,)), dma((3,)), dma, dma, dma, dma, dma, dma,
         ],
         compiler_params=pltpu.CompilerParams(collective_id=0, has_side_effects=True, vmem_limit_bytes=24 << 20),
     )(*[pltpu.with_memory_space_constraint(a, pltpu.HBM) for a in operands + scalars])
+    results = (disp_next, row, micro)
+    disp_next, row, micro = pl.pallas_call(
+        leave,
+        out_shape=tuple(jax.ShapeDtypeStruct(a.shape, a.dtype) for a in results),
+        in_specs=[pl.BlockSpec(memory_space=pl.ANY)] * 3,
+        out_specs=(pl.BlockSpec(memory_space=pltpu.HBM),) * 3,
+        scratch_shapes=[dma((3,))],
+        compiler_params=pltpu.CompilerParams(vmem_limit_bytes=1 << 20),
+    )(*results)
     return disp_next, row, micro.reshape(6, 32, 1, 1024)
 
 

time: 48.2 us -> 39.6 us (0.82)
  Pallas kernels: 45.4 us -> 38.8 us
  local copies, waits for them, and re-layouts: 2.03 us -> 0 us
    pallas_call x1, Pallas kernels: 45.4 us -> 37.9 us  [shards(): pl.pallas_call(kernel, out_shape=(jax.ShapeDtypeStruct(displacement.shape...]
    unnamed x3 -> x0, local copies, waits for them, and re-layouts: 2.03 us -> none
    pallas_call x0 -> x1, Pallas kernels: none -> 0.93 us  [shards(): pl.pallas_call(leave, out_shape=tuple((jax.ShapeDtypeStruct(a.shape, a.dt...]
where the time goes in v2:
time: 39.6 us; the launch traced here: 39.5 us
  Pallas kernels  38.8 us (98%)
  between operations  0.64 us (2%)
    pallas_call x1, Pallas kernels, shards(): pl.pallas_call(kernel, out_shape=(jax.ShapeDtypeStruct(displacement.shape...  37.9 us
    pallas_call x1, Pallas kernels, shards(): pl.pallas_call(leave, out_shape=tuple((jax.ShapeDtypeStruct(a.shape, a.dt...  0.93 us

profile of v2, /device:TPU:1, one launch (start us, length us, event | category | flops | bytes accessed | tf_op | source)
XLA Modules:
  0.0 39.5 jit_solution(5462263739472856114)
XLA Ops:
  0.6 37.9 %shard_map.139 = (f32[3,2,32,32]{3,2,1,0:T(8,128)S(1)}, f32[1,8]{1,0:T(1,128)S(1)}, f32[1536,128]{1,0:T(8,128)S(1)}) custom-call(f32[3,2,32,32]{3,2,1,0:T(8,128)} %disp_in.1, f32[4,32,512]{2,1,0:T(8,128)} %constant.10.clone.wt_in, bf16[32,1024]{1,0:T(8,128)(2,1)} %bitcast.3, bf16[32,1024]{1,0:T(8,128)(2,1)} %bitcast.4, f32[3,2,32,32]{3,2,1,0:T(8,128)} %force_in.1, ...), custom_call_target="tpu_custom_call" | custom-call | tf_op jit(solution)/shard_map/pallas_call | solution.py:755
  38.5 0.9 %shard_map.140 = (f32[3,2,32,32]{3,2,1,0:T(8,128)}, f32[1,8]{1,0:T(1,128)}, f32[1536,128]{1,0:T(8,128)}) custom-call(f32[3,2,32,32]{3,2,1,0:T(8,128)S(1)} %get-tuple-element.9.a, f32[1,8]{1,0:T(1,128)S(1)} %get-tuple-element.10.b, f32[1536,128]{1,0:T(8,128)S(1)} %get-tuple-element.11.c), custom_call_target="tpu_custom_call" | custom-call | tf_op jit(solution)/shard_map/pallas_call | solution.py:802

commit v3 on v2

--- a/solution.py
+++ b/solution.py
@@ -8,6 +8,7 @@
 
 VOX = 32
 HALF = 512
+PIECES = 2
 KMAX = 4
 MESH = pl.DeviceIdType.MESH
 NEAR = (-2, -1, 1, 2)
@@ -55,7 +56,7 @@
     weight = np.where(kz == 0, 1.0, 2.0)[None] * one
     scaled = -(1.0 / shear_ref) * inverse * weight / VOX**3
     pairs = (xx * xx, xy * xy, xz * xz, 2 * xy * xz, 2 * xx * xz, 2 * xx * xy)
-    spectral = np.stack([scaled] + [green_ratio * p * inverse for p in pairs])
+    spectral = np.stack([scaled] + [green_ratio * p * inverse for p in pairs] + [xx, xy, xz])
     to = lambda a: np.asarray(a, np.float32)
     return (
         to(np.stack([cy, sy, zr, zi])),
@@ -111,13 +112,6 @@
     moved = roll(v, VOX, 2)
     last_row = jnp.where(row_of(v.shape) == 0, 0.0, roll(moved, 1, 1))
     return jnp.where(lane_of(v.shape) >= VOX, moved, last_row)
-
-
-def zc(v):
-    lane = lane_of(v.shape) % VOX
-    up = jnp.where(lane == VOX - 1, roll(v, 31, 2), roll(v, -1, 2))
-    down = jnp.where(lane == 0, roll(v, -31, 2), roll(v, 1, 2))
-    return 0.5 * (up - down)
 
 
 def yc(v):
@@ -163,11 +157,11 @@
     xx, yy, zz, yz, xz, xy = stress
     result = []
     for along_x, along_y, along_z in ((xx, xy, xz), (xy, yy, yz), (xz, yz, zz)):
-        smooth_x = 0.5 * (along_x + z_down(along_x))
-        first = 0.5 * (smooth_x + y_down(smooth_x))
-        smooth_y = 0.5 * (along_y + z_down(along_y))
-        slope_z = z_down(along_z) - along_z
-        rest = (y_down(smooth_y) - smooth_y) + 0.5 * (slope_z + y_down(slope_z))
+        smooth = along_x + z_down(along_x)
+        first = 0.25 * (smooth + y_down(smooth))
+        both = along_y + along_z
+        less = along_z - along_y
+        rest = y_down(0.5 * (z_down(both) - less)) + 0.5 * (z_down(less) - both)
         result.append((first[:-1] - first[1:]) + 0.5 * (rest[1:] + rest[:-1]))
     return result
 
@@ -197,10 +191,10 @@
     disp_raw, wt_ref, lame_raw, shear_raw, force_raw, samp_raw, vt_ref, vz_ref, x_ref, spec_ref,
     steps_ref, slot_ref, in_sem,
     disp_ref, force_ref, samp_ref, mod_ref, modwide,
-    nb_first, nb_disp, nb_force, nb_samp, modbuf, part, partbuf, strainrow,
-    wh, wl, vh, vl, field, pot, disp_u, gam, flu, flubuf,
+    nb_first, nb_disp, nb_force, nb_samp, modbuf, part, partbuf, strainrow, one_hot_ref,
+    wh, wl, vh, vl, field, disp_u, gam, flu, flubuf,
     rowbuf, joined, respbuf, moment, momentbuf,
-    first_sem, near_send, near_recv, mod_send, mod_recv, part_send, part_recv,
+    ready, first_sem, near_send, near_recv, mod_send, mod_recv, part_send, part_recv,
     y_send, y_recv, resp_send, resp_recv, flu_send, flu_recv, mom_send, mom_recv,
 ):
     me = lax.axis_index("dev")
@@ -223,25 +217,45 @@
             )
         )
     ]
-    for copy in loads:
-        copy.start()
+    loads[0].start()
 
     barrier = pltpu.get_barrier_semaphore()
-
-    for peer in peers:
+    layer = [peer for peer, (a, _, _) in zip(peers, OTHERS) if a == 0]
+    entry = [peer for peer, (_, b, c) in zip(peers, OTHERS) if (b, c) == (0, 0)] + layer
+    entry.append(lax.rem(me + 1, 32))
+    for peer in entry:
         pl.semaphore_signal(barrier, inc=1, device_id={"dev": peer}, device_id_type=MESH)
     for i in range(1, 4):
         pl.semaphore_signal(
             barrier, inc=1, device_id={"grp": lax.rem(group + i, 4)}, device_id_type=MESH
         )
-
-    for k in (0, 2, 3, 4, 5):
-        loads[k].wait()
-    for raw, dense in ((disp_raw, disp_ref), (force_raw, force_ref), (samp_raw, samp_ref)):
+    for copy in loads[1:]:
+        copy.start()
+
+    def dense(raw, out):
         for index in np.ndindex(raw.shape[:-2]):
-            dense[index] = jnp.concatenate(
+            out[index] = jnp.concatenate(
                 [raw[(*index, pl.ds(q, 8, stride=4), slice(None))] for q in range(4)], axis=1
             )
+
+    loads[0].wait()
+    dense(disp_raw, disp_ref)
+    pl.semaphore_wait(barrier, len(entry) + 3)
+    first_plane = pltpu.make_async_remote_copy(
+        src_ref=disp_ref.at[:, 0],
+        dst_ref=nb_first,
+        send_sem=first_sem.at[0],
+        recv_sem=first_sem.at[1],
+        device_id={"dev": lax.rem(me + 31, 32)},
+        device_id_type=MESH,
+    )
+    first_plane.start()
+    for peer in layer:
+        pl.semaphore_signal(ready, inc=1, device_id={"dev": peer}, device_id_type=MESH)
+    for k in range(2, 6):
+        loads[k].wait()
+    dense(force_raw, force_ref)
+    dense(samp_raw, samp_ref)
     for k, raw in enumerate((lame_raw, shear_raw)):
         wide = raw[...].astype(f32)
         for t in range(8):
@@ -250,7 +264,9 @@
         mod_ref[r] = modwide[pl.ds(r * 16, 16), :].astype(bf16)
 
     part[...] = jnp.zeros_like(part)
-    pl.semaphore_wait(barrier, 34)
+    for plane in range(count):
+        strainrow[plane, pl.ds(48, 8), :] = jnp.ones((8, 128), f32)
+        strainrow[plane, pl.ds(56, 8), :] = jnp.zeros((8, 128), f32)
 
     def near_copies(source, target, k):
         out = []
@@ -272,15 +288,6 @@
         near_copies(force_ref, nb_force, 1),
         near_copies(samp_ref, nb_samp, 2),
     ]
-    first_plane = pltpu.make_async_remote_copy(
-        src_ref=disp_ref.at[:, 0],
-        dst_ref=nb_first,
-        send_sem=first_sem.at[0],
-        recv_sem=first_sem.at[1],
-        device_id={"dev": lax.rem(me + 31, 32)},
-        device_id_type=MESH,
-    )
-    first_plane.start()
 
     def everyone(source, target, send, recv):
         for peer in peers:
@@ -297,9 +304,6 @@
         ref = target.at[pl.ds(0, 31)]
         pltpu.make_async_copy(ref, ref, recv).wait()
 
-    everyone(lambda peer: mod_ref.at[peer], modbuf, mod_send, mod_recv)
-    modbuf[me] = mod_ref[me]
-
     loads[1].wait()
 
     @pl.loop(0, 32)
@@ -312,30 +316,35 @@
             wh[rows, pl.ds(k * HALF, HALF)] = high
             wl[rows, pl.ds(k * HALF, HALF)] = low
 
+    one_hots, rows_high, rows_low = [], [], []
+    for plane in range(count):
+        sample = samp_ref[plane]
+        for s in range(8):
+            hit = jnp.broadcast_to(sample[s : s + 1], (32, 128)) == (
+                row_of((32, 128)) + group * 32
+            )
+            one_hots.append(jnp.where(hit, 1.0, 0.0).astype(bf16))
+    one_hot_ref[...] = jnp.concatenate(one_hots, axis=1)
+    pl.semaphore_wait(ready, len(layer))
+    everyone(lambda peer: mod_ref.at[peer], modbuf, mod_send, mod_recv)
+    modbuf[me] = mod_ref[me]
+
     first_plane.wait_recv()
     inside_up = (me < 31).astype(f32)
     fields = [
         jnp.concatenate([disp_ref[c], nb_first[pl.ds(c, 1)] * inside_up], axis=0) for c in range(3)
     ]
     strain = strain_of(fields)
-    one_hots, rows_high, rows_low = [], [], []
     for plane in range(count):
         for c in range(6):
             strainrow[plane, pl.ds(c * 8, 8), :] = strain[c][plane]
-        strainrow[plane, pl.ds(48, 8), :] = jnp.ones((8, 128), f32)
-        strainrow[plane, pl.ds(56, 8), :] = jnp.zeros((8, 128), f32)
     for plane in range(count):
-        sample = samp_ref[plane]
         for s in range(8):
             rows = strainrow[plane, pl.ds(s, 8, stride=8), :]
             high, low = split(rows)
             rows_high.append(high)
             rows_low.append(low)
-            hit = jnp.broadcast_to(sample[s : s + 1], (32, 128)) == (
-                row_of((32, 128)) + group * 32
-            )
-            one_hots.append(jnp.where(hit, 1.0, 0.0).astype(bf16))
-    one_hot = jnp.concatenate(one_hots, axis=1)
+    one_hot = one_hot_ref[...]
 
     def against(rows):
         return lax.dot_general(
@@ -386,21 +395,25 @@
         down = jnp.concatenate([before, v[:-1]], axis=0)
         return 0.5 * (up - down)
 
-    def forward(slot):
+    def forward():
         rows = jnp.concatenate(
-            [field[slot, pl.ds(s, 32, stride=8), :] for s in range(8)], axis=1
+            [
+                jnp.concatenate([field[k, pl.ds(s, 32, stride=8), :] for k in range(2)], axis=0)
+                for s in range(8)
+            ],
+            axis=1,
         )
         high, low = split(rows)
         both = mm(jnp.concatenate([high, low], axis=0), wh[...])
-        plane = both[:32] + (both[32:] + mm(high, wl[...]))
-        return product(x_ref[0], jnp.concatenate([plane[:, :HALF], plane[:, HALF:]], axis=0))
-
-    @pl.loop(0, 4)
-    def _(t):
-        lame, shear = moduli(t * 8, 8)
-        field[0, at(t * 8, 8), :] = (lame + (2.0 / 3.0) * shear).reshape(64, 128)
-
-    spectrum_a = forward(0)
+        plane = both[:64] + (both[64:] + mm(high, wl[...]))
+        stacked = jnp.concatenate(
+            [
+                jnp.concatenate([plane[:32, :HALF], plane[32:, :HALF]], axis=1),
+                jnp.concatenate([plane[:32, HALF:], plane[32:, HALF:]], axis=1),
+            ],
+            axis=0,
+        )
+        return product(x_ref[0], stacked)
 
     ref = partbuf.at[pl.ds(0, 31)]
     pltpu.make_async_copy(ref, ref, part_recv).wait()
@@ -420,11 +433,13 @@
 
     @pl.loop(0, 4)
     def _(t):
-        _, shear = moduli(t * 8, 8)
+        lame, shear = moduli(t * 8, 8)
+        field[0, at(t * 8, 8), :] = (lame + (2.0 / 3.0) * shear).reshape(64, 128)
         scale, _ = relaxed(shear, size, rates)
         field[1, at(t * 8, 8), :] = (2.0 * shear * scale).reshape(64, 128)
 
-    spectrum_b = forward(1)
+    spectrum = forward()
+    spectrum_a, spectrum_b = spectrum[:, :HALF], spectrum[:, HALF:]
     mix = d[0] * spec_ref[1]
     for c in range(1, 6):
         mix = mix + d[c] * spec_ref[1 + c]
@@ -435,39 +450,44 @@
         scaled * (steady * spectrum_a[:32]) - mix * phi[0],
         scaled * (steady * spectrum_a[32:]) - mix * phi[1],
     ]
+    waves = [spec_ref[7 + c] for c in range(3)]
+    turned = [
+        d[0] * waves[0] + d[5] * waves[1] + d[4] * waves[2],
+        d[5] * waves[0] + d[1] * waves[1] + d[3] * waves[2],
+        d[4] * waves[0] + d[3] * waves[1] + d[2] * waves[2],
+    ]
+    slopes = [
+        [waves[c] * pressure[k] + turned[c] * phi[k] for k in range(2)] for c in range(3)
+    ]
     mixed = jnp.concatenate(
         [
-            jnp.concatenate([pressure[0], phi[0]], axis=1),
-            jnp.concatenate([pressure[1], phi[1]], axis=1),
+            jnp.concatenate([-slopes[c][1] for c in range(3)], axis=1),
+            jnp.concatenate([slopes[c][0] for c in range(3)], axis=1),
         ],
         axis=0,
     )
     back = product(x_ref[1], mixed)
     lines = jnp.concatenate(
         [
-            jnp.concatenate([back[:32, :HALF], back[32:, :HALF]], axis=1),
-            jnp.concatenate([back[:32, HALF:], back[32:, HALF:]], axis=1),
+            jnp.concatenate([back[:32, c * HALF :][:, :HALF], back[32:, c * HALF :][:, :HALF]], axis=1)
+            for c in range(3)
         ],
         axis=0,
     )
     high, low = split(lines)
     both = mm(jnp.concatenate([high, low], axis=0), vh[...])
-    space = both[:64] + (both[64:] + mm(high, vl[...]))
-    for k in range(2):
+    space = both[:96] + (both[96:] + mm(high, vl[...]))
+    for c in range(3):
         for s in range(8):
-            pot[k, pl.ds(s, 32, stride=8), :] = space[k * 32 : k * 32 + 32, s * 128 : s * 128 + 128]
-
-    @pl.loop(0, 8)
-    def _(t):
-        x = t * 4
-        p, q = planes(pot, 0, x, 4), planes(pot, 1, x, 4)
-        px, qx = x_slope(pot, 0, x, 4, p), x_slope(pot, 1, x, 4, q)
-        py, pz, qy, qz = yc(p), zc(p), yc(q), zc(q)
-        ux = px + d[0] * qx + d[5] * qy + d[4] * qz
-        uy = py + d[5] * qx + d[1] * qy + d[3] * qz
-        uz = pz + d[4] * qx + d[3] * qy + d[2] * qz
-        for c, u in enumerate((ux, uy, uz)):
-            disp_u[c, at(x, 4), :] = u.reshape(32, 128)
+            disp_u[c, pl.ds(s, 32, stride=8), :] = space[
+                c * 32 : c * 32 + 32, s * 128 : s * 128 + 128
+            ]
+
+    source, target = row_of((128, 128)), lane_of((128, 128))
+    line = source // VOX == target // VOX
+    ahead = line & ((target + 1) % VOX == source % VOX)
+    behind = line & ((target + VOX - 1) % VOX == source % VOX)
+    z_matrix = (jnp.where(ahead, 0.5, 0.0) - jnp.where(behind, 0.5, 0.0)).astype(bf16)
 
     def send_planes(t):
         for b, c in sorted(((b, c) for b in range(4) for c in range(2)), key=lambda p: -spans(p[0])):
@@ -493,12 +513,14 @@
         x = lax.rem(me_x + 2 + t, 4) * 8
         ux, uy, uz = (planes(disp_u, c, x, 8) for c in range(3))
         dx = [x_slope(disp_u, c, x, 8, u) for c, u in enumerate((ux, uy, uz))]
+        high, low = split(jnp.concatenate([ux, uy, uz], axis=0).reshape(192, 128))
+        dz = (mm(high, z_matrix) + mm(low, z_matrix)).reshape(3, 8, 8, 128)
         change = [
             -dx[0],
             -yc(uy),
-            -zc(uz),
-            -0.5 * (yc(uz) + zc(uy)),
-            -0.5 * (dx[2] + zc(ux)),
+            -dz[2],
+            -0.5 * (yc(uz) + dz[1]),
+            -0.5 * (dx[2] + dz[0]),
             -0.5 * (dx[1] + yc(ux)),
         ]
         for c in range(6):
@@ -720,10 +742,10 @@
 
 
 def leave(a, b, c, a_out, b_out, c_out, sem):
-    copies = [
-        pltpu.make_async_copy(source, target, sem.at[k])
-        for k, (source, target) in enumerate(((c, c_out), (a, a_out), (b, b_out)))
-    ]
+    step = c.shape[0] // PIECES
+    pairs = [(a, a_out), (b, b_out)]
+    pairs += [(c.at[pl.ds(k * step, step)], c_out.at[pl.ds(k * step, step)]) for k in range(PIECES)]
+    copies = [pltpu.make_async_copy(*pair, sem.at[k]) for k, pair in enumerate(pairs)]
     for copy in copies:
         copy.start()
     for copy in copies:
@@ -778,11 +800,11 @@
             pltpu.VMEM((32, 1, 128), f32),
             pltpu.VMEM((32, 1, 128), f32),
             pltpu.VMEM((count, 64, 128), f32),
+            pltpu.VMEM((32, count * 1024), bf16),
             pltpu.VMEM((1024, 1024), bf16),
             pltpu.VMEM((1024, 1024), bf16),
             pltpu.VMEM((1024, 1024), bf16),
             pltpu.VMEM((1024, 1024), bf16),
-            pltpu.VMEM((2, 256, 128), f32),
             pltpu.VMEM((2, 256, 128), f32),
             pltpu.VMEM((3, 256, 128), f32),
             pltpu.VMEM((6, 256, 128), f32),
@@ -793,7 +815,7 @@
             pltpu.VMEM((32, 1, 128), f32),
             pltpu.VMEM((1, 1, 128), f32),
             pltpu.VMEM((32, 1, 128), f32),
-            dma((2,)), dma((3, 4)), dma((3, 4)), dma, dma, dma, dma,
+            pltpu.SemaphoreType.REGULAR, dma((2,)), dma((3, 4)), dma((3, 4)), dma, dma, dma, dma,
             dma((3,)), dma((3,)), dma, dma, dma, dma, dma, dma,
         ],
         compiler_params=pltpu.CompilerParams(collective_id=0, has_side_effects=True, vmem_limit_bytes=24 << 20),
@@ -804,7 +826,7 @@
         out_shape=tuple(jax.ShapeDtypeStruct(a.shape, a.dtype) for a in results),
         in_specs=[pl.BlockSpec(memory_space=pl.ANY)] * 3,
         out_specs=(pl.BlockSpec(memory_space=pltpu.HBM),) * 3,
-        scratch_shapes=[dma((3,))],
+        scratch_shapes=[dma((PIECES + 2,))],
         compiler_params=pltpu.CompilerParams(vmem_limit_bytes=1 << 20),
     )(*results)
     return disp_next, row, micro.reshape(6, 32, 1, 1024)

time: 39.6 us -> 37.3 us (0.942)
  Pallas kernels: 38.8 us -> 36.5 us
    pallas_call x1, Pallas kernels: 37.9 us -> 35.6 us  [shards(): pl.pallas_call(kernel, out_shape=(jax.ShapeDtypeStruct(displacement.shape...]
where the time goes in v3:
time: 37.3 us; the launch traced here: 37.1 us
  Pallas kernels  36.5 us (98%)
  between operations  0.64 us (2%)
    pallas_call x1, Pallas kernels, shards(): pl.pallas_call(kernel, out_shape=(jax.ShapeDtypeStruct(displacement.shape...  35.6 us
    pallas_call x1, Pallas kernels, shards(): pl.pallas_call(leave, out_shape=tuple((jax.ShapeDtypeStruct(a.shape, a.dt...  0.95 us

profile of v3, /device:TPU:1, one launch (start us, length us, event | category | flops | bytes accessed | tf_op | source)
XLA Modules:
  0.0 37.1 jit_solution(18015011334608301595)
XLA Ops:
  0.6 35.6 %shard_map.139 = (f32[3,2,32,32]{3,2,1,0:T(8,128)S(1)}, f32[1,8]{1,0:T(1,128)S(1)}, f32[1536,128]{1,0:T(8,128)S(1)}) custom-call(f32[3,2,32,32]{3,2,1,0:T(8,128)} %disp_in.1, f32[4,32,512]{2,1,0:T(8,128)} %constant.10.clone.wt_in, bf16[32,1024]{1,0:T(8,128)(2,1)} %bitcast.3, bf16[32,1024]{1,0:T(8,128)(2,1)} %bitcast.4, f32[3,2,32,32]{3,2,1,0:T(8,128)} %force_in.1, ...), custom_call_target="tpu_custom_call" | custom-call | tf_op jit(solution)/shard_map/pallas_call | solution.py:777
  36.2 0.9 %shard_map.140 = (f32[3,2,32,32]{3,2,1,0:T(8,128)}, f32[1,8]{1,0:T(1,128)}, f32[1536,128]{1,0:T(8,128)}) custom-call(f32[3,2,32,32]{3,2,1,0:T(8,128)S(1)} %get-tuple-element.9.a, f32[1,8]{1,0:T(1,128)S(1)} %get-tuple-element.10.b, f32[1536,128]{1,0:T(8,128)S(1)} %get-tuple-element.11.c), custom_call_target="tpu_custom_call" | custom-call | tf_op jit(solution)/shard_map/pallas_call | solution.py:824

commit v4 on v3

--- a/solution.py
+++ b/solution.py
@@ -249,7 +249,7 @@
         device_id={"dev": lax.rem(me + 31, 32)},
         device_id_type=MESH,
     )
-    first_plane.start()
+    pl.when(me > 0)(first_plane.start)
     for peer in layer:
         pl.semaphore_signal(ready, inc=1, device_id={"dev": peer}, device_id_type=MESH)
     for k in range(2, 6):
@@ -268,26 +268,25 @@
         strainrow[plane, pl.ds(48, 8), :] = jnp.ones((8, 128), f32)
         strainrow[plane, pl.ds(56, 8), :] = jnp.zeros((8, 128), f32)
 
-    def near_copies(source, target, k):
-        out = []
+    near = []
+    for k, (source, target) in enumerate(
+        ((disp_ref, nb_disp), (force_ref, nb_force), (samp_ref, nb_samp))
+    ):
         for o, offset in enumerate(NEAR):
-            out.append(
+            if offset == 2 and k < 2:
+                continue
+            part_of = pl.ds(0 if offset == -2 else count - 1, 1) if abs(offset) == 2 else pl.ds(0, count)
+            index = (part_of,) if k == 2 else (slice(None), part_of)
+            near.append(
                 pltpu.make_async_remote_copy(
-                    src_ref=source,
-                    dst_ref=target.at[3 - o],
+                    src_ref=source.at[index],
+                    dst_ref=target.at[(3 - o, *index)],
                     send_sem=near_send.at[k, o],
                     recv_sem=near_recv.at[k, 3 - o],
                     device_id={"dev": lax.rem(me + offset + 32, 32)},
                     device_id_type=MESH,
                 )
             )
-        return out
-
-    near = [
-        near_copies(disp_ref, nb_disp, 0),
-        near_copies(force_ref, nb_force, 1),
-        near_copies(samp_ref, nb_samp, 2),
-    ]
 
     def everyone(source, target, send, recv):
         for peer in peers:
@@ -329,10 +328,9 @@
     everyone(lambda peer: mod_ref.at[peer], modbuf, mod_send, mod_recv)
     modbuf[me] = mod_ref[me]
 
-    first_plane.wait_recv()
-    inside_up = (me < 31).astype(f32)
+    pl.when(me < 31)(first_plane.wait_recv)
     fields = [
-        jnp.concatenate([disp_ref[c], nb_first[pl.ds(c, 1)] * inside_up], axis=0) for c in range(3)
+        jnp.concatenate([disp_ref[c], jnp.where(me < 31, nb_first[pl.ds(c, 1)], 0.0)], axis=0) for c in range(3)
     ]
     strain = strain_of(fields)
     for plane in range(count):
@@ -359,9 +357,6 @@
         part[r, :, pl.ds(0, 8)] = sums[r : r + 1]
     everyone(lambda peer: part.at[peer], partbuf, part_send, part_recv)
     partbuf[me] = part[me]
-    for k in range(3):
-        for copy in near[k]:
-            copy.start()
     for k in range(6, 12):
         loads[k].wait()
 
@@ -417,6 +412,8 @@
 
     ref = partbuf.at[pl.ds(0, 31)]
     pltpu.make_async_copy(ref, ref, part_recv).wait()
+    for copy in near:
+        copy.start()
     total = jnp.sum(partbuf[...], axis=0)
     lane1 = lane_of((1, 128))
 
@@ -575,17 +572,16 @@
     everyone(lambda peer: joined.at[0], respbuf, resp_send, resp_recv)
     respbuf[me] = joined[0]
 
-    for k in range(3):
-        for o in range(4):
-            ref = (nb_disp, nb_force, nb_samp)[k].at[o]
-            pltpu.make_async_copy(ref, ref, near_recv.at[k, o]).wait()
+    for copy in near:
+        copy.wait_recv()
     exists = [(me * count + j >= 3).astype(f32) * (me * count + j < 67).astype(f32) for j in range(8)]
 
     def extended(own, near_ref, c):
         def get(ref, p):
             return ref[c, pl.ds(p, 1)] if c is not None else ref[pl.ds(p, 1)]
 
-        planes = [get(near_ref.at[0], 1), get(near_ref.at[1], 0), get(near_ref.at[1], 1)]
+        lowest = get(near_ref.at[0], 1) if c is None else get(near_ref.at[1], 0)
+        planes = [lowest, get(near_ref.at[1], 0), get(near_ref.at[1], 1)]
         planes += [get(own, 0), get(own, 1)]
         planes += [get(near_ref.at[2], 0), get(near_ref.at[2], 1), get(near_ref.at[3], 0)]
         return planes
@@ -727,10 +723,9 @@
             for q in range(4):
                 disp_out[c, p, pl.ds(q, 8, stride=4), :] = new[p][:, q * 32 : q * 32 + 32]
 
-    first_plane.wait_send()
-    for k in range(3):
-        for copy in near[k]:
-            copy.wait_send()
+    pl.when(me > 0)(first_plane.wait_send)
+    for copy in near:
+        copy.wait_send()
     for copy in rows_out:
         copy.wait_send()
     for buffer, sem in (

time: 37.3 us -> 36.4 us (0.976)
  Pallas kernels: 36.5 us -> 35.6 us
    pallas_call x1, Pallas kernels: 35.6 us -> 34.7 us  [shards(): pl.pallas_call(kernel, out_shape=(jax.ShapeDtypeStruct(displacement.shape...]
where the time goes in v4:
time: 36.4 us; the launch traced here: 36.3 us
  Pallas kernels  35.6 us (98%)
  between operations  0.64 us (2%)
    pallas_call x1, Pallas kernels, shards(): pl.pallas_call(kernel, out_shape=(jax.ShapeDtypeStruct(displacement.shape...  34.7 us
    pallas_call x1, Pallas kernels, shards(): pl.pallas_call(leave, out_shape=tuple((jax.ShapeDtypeStruct(a.shape, a.dt...  0.95 us

profile of v4, /device:TPU:1, one launch (start us, length us, event | category | flops | bytes accessed | tf_op | source)
XLA Modules:
  0.0 36.3 jit_solution(3505927086609869346)
XLA Ops:
  0.6 34.7 %shard_map.139 = (f32[3,2,32,32]{3,2,1,0:T(8,128)S(1)}, f32[1,8]{1,0:T(1,128)S(1)}, f32[1536,128]{1,0:T(8,128)S(1)}) custom-call(f32[3,2,32,32]{3,2,1,0:T(8,128)} %disp_in.1, f32[4,32,512]{2,1,0:T(8,128)} %constant.10.clone.wt_in, bf16[32,1024]{1,0:T(8,128)(2,1)} %bitcast.3, bf16[32,1024]{1,0:T(8,128)(2,1)} %bitcast.4, f32[3,2,32,32]{3,2,1,0:T(8,128)} %force_in.1, ...), custom_call_target="tpu_custom_call" | custom-call | tf_op jit(solution)/shard_map/pallas_call | solution.py:772
  35.3 0.9 %shard_map.140 = (f32[3,2,32,32]{3,2,1,0:T(8,128)}, f32[1,8]{1,0:T(1,128)}, f32[1536,128]{1,0:T(8,128)}) custom-call(f32[3,2,32,32]{3,2,1,0:T(8,128)S(1)} %get-tuple-element.9.a, f32[1,8]{1,0:T(1,128)S(1)} %get-tuple-element.10.b, f32[1536,128]{1,0:T(8,128)S(1)} %get-tuple-element.11.c), custom_call_target="tpu_custom_call" | custom-call | tf_op jit(solution)/shard_map/pallas_call | solution.py:819

commit v5 on v4

--- a/solution.py
+++ b/solution.py
@@ -8,7 +8,8 @@
 
 VOX = 32
 HALF = 512
-PIECES = 2
+BLOCK = 32
+PIECES = 1
 KMAX = 4
 MESH = pl.DeviceIdType.MESH
 NEAR = (-2, -1, 1, 2)
@@ -26,10 +27,11 @@
 def tables():
     n = np.arange(VOX)
     theta = 2.0 * np.pi / VOX
-    ky = np.repeat(n, 16)
+    order = np.concatenate([n[::2], n[1::2]])
+    ky = np.repeat(order, 16)
     kz = np.tile(np.arange(16), VOX)
-    yy = np.repeat(n, VOX)
-    zz = np.tile(n, VOX)
+    yy = np.repeat(n[:16], VOX)
+    zz = np.tile(n, 16)
     k16 = np.arange(16)
 
     def zeta(z, k):
@@ -41,7 +43,7 @@
 
     cy, sy = np.cos(theta * (np.outer(n, ky) % VOX)), np.sin(theta * (np.outer(n, ky) % VOX))
     zr, zi = zeta(n[:, None], kz[None, :])
-    cv, sv = np.cos(theta * (np.outer(n, yy) % VOX)), np.sin(theta * (np.outer(n, yy) % VOX))
+    cv, sv = np.cos(theta * (np.outer(order, yy) % VOX)), np.sin(theta * (np.outer(order, yy) % VOX))
     vr, vi = zeta(zz[None, :], k16[:, None])
     c, s = np.cos(theta * (np.outer(n, n) % VOX)), np.sin(theta * (np.outer(n, n) % VOX))
     x = np.block([[c, s], [-s, c]])
@@ -79,7 +81,7 @@
 def product(a, b):
     ah, al = split(a)
     bh, bl = split(b)
-    return mm(ah, bh) + (mm(al, bh) + mm(ah, bl))
+    return mm(jnp.concatenate([ah, al, ah], axis=1), jnp.concatenate([bh, bh, bl], axis=0))
 
 
 def lane_of(shape):
@@ -94,24 +96,19 @@
     return pltpu.roll(a, shift % a.shape[axis], axis)
 
 
-def z_up(v):
-    return jnp.where(lane_of(v.shape) % VOX == VOX - 1, 0.0, roll(v, -1, 2))
-
-
-def z_down(v):
-    return jnp.where(lane_of(v.shape) % VOX == 0, 0.0, roll(v, 1, 2))
-
-
-def y_up(v):
-    moved = roll(v, -VOX, 2)
-    next_row = jnp.where(row_of(v.shape) == 7, 0.0, roll(moved, -1, 1))
-    return jnp.where(lane_of(v.shape) < 96, moved, next_row)
-
-
-def y_down(v):
-    moved = roll(v, VOX, 2)
-    last_row = jnp.where(row_of(v.shape) == 0, 0.0, roll(moved, 1, 1))
-    return jnp.where(lane_of(v.shape) >= VOX, moved, last_row)
+def shifts(v, sign):
+    lane, row = lane_of(v.shape), row_of(v.shape)
+    edge = lane % VOX == (VOX - 1 if sign > 0 else 0)
+    inner = lane < 96 if sign > 0 else lane >= VOX
+    last = row == (7 if sign > 0 else 0)
+
+    def along_y(moved):
+        return jnp.where(inner, moved, jnp.where(last, 0.0, roll(moved, -sign, 1)))
+
+    z = jnp.where(edge, 0.0, roll(v, -sign, 2))
+    y = along_y(roll(v, -sign * VOX, 2))
+    both = jnp.where(edge, 0.0, along_y(roll(v, -sign * (VOX + 1), 2)))
+    return z, y, both
 
 
 def yc(v):
@@ -136,11 +133,10 @@
 def strain_of(fields):
     slopes = []
     for w in fields:
-        up = z_up(w)
-        mz, dz = 0.5 * (w + up), up - w
-        moved = y_up(mz)
-        a, b = 0.5 * (mz + moved), moved - mz
-        c = 0.5 * (dz + y_up(dz))
+        z, y, yz = shifts(w, 1)
+        near, far = w + z, y + yz
+        a, b = 0.25 * (near + far), 0.5 * (far - near)
+        c = 0.5 * ((z + yz) - (w + y))
         slopes.append((a[1:] - a[:-1], 0.5 * (b[1:] + b[:-1]), 0.5 * (c[1:] + c[:-1])))
     x, y, z = slopes
     return (
@@ -157,11 +153,13 @@
     xx, yy, zz, yz, xz, xy = stress
     result = []
     for along_x, along_y, along_z in ((xx, xy, xz), (xy, yy, yz), (xz, yz, zz)):
-        smooth = along_x + z_down(along_x)
-        first = 0.25 * (smooth + y_down(smooth))
+        z, y, yz = shifts(along_x, -1)
+        first = 0.25 * ((along_x + z) + (y + yz))
         both = along_y + along_z
         less = along_z - along_y
-        rest = y_down(0.5 * (z_down(both) - less)) + 0.5 * (z_down(less) - both)
+        z, y, _ = shifts(less, -1)
+        _, _, yz = shifts(both, -1)
+        rest = 0.5 * ((yz - y) + (z - both))
         result.append((first[:-1] - first[1:]) + 0.5 * (rest[1:] + rest[:-1]))
     return result
 
@@ -192,7 +190,7 @@
     steps_ref, slot_ref, in_sem,
     disp_ref, force_ref, samp_ref, mod_ref, modwide,
     nb_first, nb_disp, nb_force, nb_samp, modbuf, part, partbuf, strainrow, one_hot_ref,
-    wh, wl, vh, vl, field, disp_u, gam, flu, flubuf,
+    wh, wl, vh, vl, field, disp_u, flu, flubuf,
     rowbuf, joined, respbuf, moment, momentbuf,
     ready, first_sem, near_send, near_recv, mod_send, mod_recv, part_send, part_recv,
     y_send, y_recv, resp_send, resp_recv, flu_send, flu_recv, mom_send, mom_recv,
@@ -305,15 +303,17 @@
 
     loads[1].wait()
 
-    @pl.loop(0, 32)
+    @pl.loop(0, 16)
     def _(y):
         c, s = wt_ref[0, pl.ds(y, 1), :], wt_ref[1, pl.ds(y, 1), :]
         zr, zi = wt_ref[2], wt_ref[3]
         rows = pl.ds(pl.multiple_of(y * 32, 32), 32)
         for k, block in enumerate((c * zr + s * zi, c * zi - s * zr)):
             high, low = split(block)
-            wh[rows, pl.ds(k * HALF, HALF)] = high
-            wl[rows, pl.ds(k * HALF, HALF)] = low
+            for odd in range(2):
+                lanes = slice(odd * 256, odd * 256 + 256)
+                wh[odd, rows, pl.ds(k * 256, 256)] = high[:, lanes]
+                wl[odd, rows, pl.ds(k * 256, 256)] = low[:, lanes]
 
     one_hots, rows_high, rows_low = [], [], []
     for plane in range(count):
@@ -360,15 +360,18 @@
     for k in range(6, 12):
         loads[k].wait()
 
-    @pl.loop(0, 32)
-    def _(k):
-        c, s = vt_ref[0, pl.ds(k, 1), :], vt_ref[1, pl.ds(k, 1), :]
-        zr, zi = vz_ref[0], vz_ref[1]
-        for p, block in enumerate((c * zr + s * zi, c * zi - s * zr)):
-            rows = pl.ds(pl.multiple_of(p * HALF + k * 16, 16), 16)
-            high, low = split(block)
-            vh[rows, :] = high
-            vl[rows, :] = low
+    for odd in range(2):
+
+        @pl.loop(0, 16)
+        def _(k):
+            row = pl.ds(odd * 16 + k, 1)
+            c, s = vt_ref[0, row, :], vt_ref[1, row, :]
+            zr, zi = vz_ref[0], vz_ref[1]
+            for p, block in enumerate((c * zr + s * zi, c * zi - s * zr)):
+                rows = pl.ds(pl.multiple_of(p * 256 + k * 16, 16), 16)
+                high, low = split(block)
+                vh[odd, rows, :] = high
+                vl[odd, rows, :] = low
 
     ref = modbuf.at[pl.ds(0, 31)]
     pltpu.make_async_copy(ref, ref, mod_recv).wait()
@@ -398,9 +401,15 @@
             ],
             axis=1,
         )
-        high, low = split(rows)
-        both = mm(jnp.concatenate([high, low], axis=0), wh[...])
-        plane = both[:64] + (both[64:] + mm(high, wl[...]))
+        halves = [rows[:, :HALF] + rows[:, HALF:], rows[:, :HALF] - rows[:, HALF:]]
+        sides = []
+        for odd, half in enumerate(halves):
+            high, low = split(half)
+            both = mm(jnp.concatenate([high, low], axis=0), wh[odd])
+            sides.append(both[:64] + (both[64:] + mm(high, wl[odd])))
+        plane = jnp.concatenate(
+            [sides[0][:, :256], sides[1][:, :256], sides[0][:, 256:], sides[1][:, 256:]], axis=1
+        )
         stacked = jnp.concatenate(
             [
                 jnp.concatenate([plane[:32, :HALF], plane[32:, :HALF]], axis=1),
@@ -464,16 +473,21 @@
         axis=0,
     )
     back = product(x_ref[1], mixed)
-    lines = jnp.concatenate(
-        [
-            jnp.concatenate([back[:32, c * HALF :][:, :HALF], back[32:, c * HALF :][:, :HALF]], axis=1)
-            for c in range(3)
-        ],
-        axis=0,
-    )
-    high, low = split(lines)
-    both = mm(jnp.concatenate([high, low], axis=0), vh[...])
-    space = both[:96] + (both[96:] + mm(high, vl[...]))
+    sides = []
+    for odd in range(2):
+        lines = jnp.concatenate(
+            [
+                jnp.concatenate(
+                    [back[h : h + 32, c * HALF + odd * 256 :][:, :256] for h in (0, 32)], axis=1
+                )
+                for c in range(3)
+            ],
+            axis=0,
+        )
+        high, low = split(lines)
+        both = mm(jnp.concatenate([high, low], axis=0), vh[odd])
+        sides.append(both[:96] + (both[96:] + mm(high, vl[odd])))
+    space = jnp.concatenate([sides[0] + sides[1], sides[0] - sides[1]], axis=1)
     for c in range(3):
         for s in range(8):
             disp_u[c, pl.ds(s, 32, stride=8), :] = space[
@@ -486,32 +500,12 @@
     behind = line & ((target + VOX - 1) % VOX == source % VOX)
     z_matrix = (jnp.where(ahead, 0.5, 0.0) - jnp.where(behind, 0.5, 0.0)).astype(bf16)
 
-    def send_planes(t):
-        for b, c in sorted(((b, c) for b in range(4) for c in range(2)), key=lambda p: -spans(p[0])):
-            peer = lax.rem(me_x + 2 + t, 4) * 8 + at_z[b] + at_c[c]
-
-            def start(peer=peer):
-                pltpu.make_async_remote_copy(
-                    src_ref=flu.at[peer],
-                    dst_ref=flubuf.at[me],
-                    send_sem=flu_send,
-                    recv_sem=flu_recv,
-                    device_id={"dev": peer},
-                    device_id_type=MESH,
-                ).start()
-
-            if (b, c) == (0, 0):
-                pl.when(t != 2)(start)
-            else:
-                start()
-
-    @pl.loop(0, 4)
-    def _(t):
-        x = lax.rem(me_x + 2 + t, 4) * 8
-        ux, uy, uz = (planes(disp_u, c, x, 8) for c in range(3))
-        dx = [x_slope(disp_u, c, x, 8, u) for c, u in enumerate((ux, uy, uz))]
-        high, low = split(jnp.concatenate([ux, uy, uz], axis=0).reshape(192, 128))
-        dz = (mm(high, z_matrix) + mm(low, z_matrix)).reshape(3, 8, 8, 128)
+    def voxel(t, sums):
+        x = t * BLOCK
+        ux, uy, uz = (planes(disp_u, c, x, BLOCK) for c in range(3))
+        dx = [x_slope(disp_u, c, x, BLOCK, u) for c, u in enumerate((ux, uy, uz))]
+        high, low = split(jnp.concatenate([ux, uy, uz], axis=0).reshape(24 * BLOCK, 128))
+        dz = (mm(high, z_matrix) + mm(low, z_matrix)).reshape(3, BLOCK, 8, 128)
         change = [
             -dx[0],
             -yc(uy),
@@ -520,19 +514,11 @@
             -0.5 * (dx[2] + dz[0]),
             -0.5 * (dx[1] + yc(ux)),
         ]
-        for c in range(6):
-            gam[c, at(x, 8), :] = change[c].reshape(64, 128)
         for k in range(3):
             pair = jnp.concatenate(change[2 * k : 2 * k + 2], axis=1)
-            flu[pl.ds(x, 8), pl.ds(k * 16, 16), :] = pair.astype(wire)
-        send_planes(t)
-
-    flubuf[me] = flu[me]
-
-    def voxel(t, sums):
-        x = t * 4
-        lame, shear = moduli(x, 4)
-        e = [load[c] + planes(gam, c, x, 4) for c in range(6)]
+            flu[pl.ds(x, BLOCK), pl.ds(k * 16, 16), :] = pair.astype(wire)
+        lame, shear = moduli(x, BLOCK)
+        e = [load[c] + change[c] for c in range(6)]
         tr = e[0] + e[1] + e[2]
         dv = [e[c] - tr / 3.0 if c < 3 else e[c] for c in range(6)]
         scale, f = relaxed(shear, norm_of(dv), rates)
@@ -542,7 +528,8 @@
         new += [lame, shear / (1.0 + f)]
         return tuple(a + jnp.sum(b, axis=0) for a, b in zip(sums, new))
 
-    sums = lax.fori_loop(0, 8, voxel, tuple(jnp.zeros((8, 128), f32) for _ in range(8)))
+    zero = jnp.zeros((8, 128), f32)
+    sums = lax.fori_loop(0, 32 // BLOCK, voxel, (zero,) * 8)
     column = jnp.concatenate([jnp.sum(a, axis=0, keepdims=True) for a in sums], axis=0)
     column = jnp.sum(column, axis=1, keepdims=True) * (1.0 / VOX**3)
     lane8, row8 = lane_of((8, 128)), row_of((8, 128))
@@ -571,6 +558,8 @@
     joined[0] = rowbuf[0] + rowbuf[1] + rowbuf[2] + rowbuf[3]
     everyone(lambda peer: joined.at[0], respbuf, resp_send, resp_recv)
     respbuf[me] = joined[0]
+    everyone(lambda peer: flu.at[peer], flubuf, flu_send, flu_recv)
+    flubuf[me] = flu[me]
 
     for copy in near:
         copy.wait_recv()
@@ -591,6 +580,11 @@
 
     around = [masked(extended(disp_ref, nb_disp, c)) for c in range(3)]
     outside = [masked(extended(force_ref, nb_force, c)) for c in range(3)]
+    given = [
+        (outside[c][1:] - spring_rate * around[c][1:])
+        * jnp.concatenate([jnp.full((1, 8, 128), m) for m in exists[1:]], axis=0)
+        for c in range(3)
+    ]
     samples = extended(samp_ref, nb_samp, None)
 
     all_arrived(respbuf, resp_recv)
@@ -612,11 +606,8 @@
         )
     lame, shear = cells[6], cells[7]
     pull = force_of(cells[:6])
-    res = [
-        (outside[c][1:] - pull[c] - spring_rate * around[c][1:])
-        * jnp.concatenate([jnp.full((1, 8, 128), m) for m in exists[1:]], axis=0)
-        for c in range(3)
-    ]
+    inside = jnp.concatenate([jnp.full((1, 8, 128), m) for m in exists[1:]], axis=0)
+    res = [given[c] - pull[c] * inside for c in range(3)]
 
     def stiff(w, low):
         n = w[0].shape[0]
@@ -796,13 +787,9 @@
             pltpu.VMEM((32, 1, 128), f32),
             pltpu.VMEM((count, 64, 128), f32),
             pltpu.VMEM((32, count * 1024), bf16),
-            pltpu.VMEM((1024, 1024), bf16),
-            pltpu.VMEM((1024, 1024), bf16),
-            pltpu.VMEM((1024, 1024), bf16),
-            pltpu.VMEM((1024, 1024), bf16),
+            *(pltpu.VMEM((2, HALF, HALF), bf16),) * 4,
             pltpu.VMEM((2, 256, 128), f32),
             pltpu.VMEM((3, 256, 128), f32),
-            pltpu.VMEM((6, 256, 128), f32),
             pltpu.VMEM((32, 48, 128), wire),
             pltpu.VMEM((32, 48, 128), wire),
             pltpu.VMEM((4, 1, 128), f32),

time: 36.4 us -> 34.5 us (0.948)
  Pallas kernels: 35.6 us -> 33.7 us
    pallas_call x1, Pallas kernels: 34.7 us -> 32.8 us  [shards(): pl.pallas_call(kernel, out_shape=(jax.ShapeDtypeStruct(displacement.shape...]
where the time goes in v5:
time: 34.5 us; the launch traced here: 34.3 us
  Pallas kernels  33.7 us (98%)
  between operations  0.64 us (2%)
    pallas_call x1, Pallas kernels, shards(): pl.pallas_call(kernel, out_shape=(jax.ShapeDtypeStruct(displacement.shape...  32.8 us
    pallas_call x1, Pallas kernels, shards(): pl.pallas_call(leave, out_shape=tuple((jax.ShapeDtypeStruct(a.shape, a.dt...  0.94 us

profile of v5, /device:TPU:1, one launch (start us, length us, event | category | flops | bytes accessed | tf_op | source)
XLA Modules:
  0.0 34.3 jit_solution(6419728171630631398)
XLA Ops:
  0.6 32.8 %shard_map.139 = (f32[3,2,32,32]{3,2,1,0:T(8,128)S(1)}, f32[1,8]{1,0:T(1,128)S(1)}, f32[1536,128]{1,0:T(8,128)S(1)}) custom-call(f32[3,2,32,32]{3,2,1,0:T(8,128)} %disp_in.1, f32[4,32,512]{2,1,0:T(8,128)} %constant.10.clone.wt_in, bf16[32,1024]{1,0:T(8,128)(2,1)} %bitcast.3, bf16[32,1024]{1,0:T(8,128)(2,1)} %bitcast.4, f32[3,2,32,32]{3,2,1,0:T(8,128)} %force_in.1, ...), custom_call_target="tpu_custom_call" | custom-call | tf_op jit(solution)/shard_map/pallas_call | solution.py:763
  33.4 0.9 %shard_map.140 = (f32[3,2,32,32]{3,2,1,0:T(8,128)}, f32[1,8]{1,0:T(1,128)}, f32[1536,128]{1,0:T(8,128)}) custom-call(f32[3,2,32,32]{3,2,1,0:T(8,128)S(1)} %get-tuple-element.9.a, f32[1,8]{1,0:T(1,128)S(1)} %get-tuple-element.10.b, f32[1536,128]{1,0:T(8,128)S(1)} %get-tuple-element.11.c), custom_call_target="tpu_custom_call" | custom-call | tf_op jit(solution)/shard_map/pallas_call | solution.py:806

commit v6 on v5

--- a/solution.py
+++ b/solution.py
@@ -189,10 +189,10 @@
     disp_raw, wt_ref, lame_raw, shear_raw, force_raw, samp_raw, vt_ref, vz_ref, x_ref, spec_ref,
     steps_ref, slot_ref, in_sem,
     disp_ref, force_ref, samp_ref, mod_ref, modwide,
-    nb_first, nb_disp, nb_force, nb_samp, modbuf, part, partbuf, strainrow, one_hot_ref,
+    nb_first, nb_last, nb_mark, nb_disp, nb_force, nb_samp, modbuf, part, partbuf, strainrow, one_hot_ref, sums_ref,
     wh, wl, vh, vl, field, disp_u, flu, flubuf,
     rowbuf, joined, respbuf, moment, momentbuf,
-    ready, first_sem, near_send, near_recv, mod_send, mod_recv, part_send, part_recv,
+    ready, first_send, first_recv, near_send, near_recv, mod_send, mod_recv, part_send, part_recv,
     y_send, y_recv, resp_send, resp_recv, flu_send, flu_recv, mom_send, mom_recv,
 ):
     me = lax.axis_index("dev")
@@ -216,19 +216,20 @@
         )
     ]
     loads[0].start()
+    loads[5].start()
 
     barrier = pltpu.get_barrier_semaphore()
     layer = [peer for peer, (a, _, _) in zip(peers, OTHERS) if a == 0]
     entry = [peer for peer, (_, b, c) in zip(peers, OTHERS) if (b, c) == (0, 0)] + layer
-    entry.append(lax.rem(me + 1, 32))
+    entry += [lax.rem(me + 1, 32), lax.rem(me + 31, 32)]
     for peer in entry:
         pl.semaphore_signal(barrier, inc=1, device_id={"dev": peer}, device_id_type=MESH)
     for i in range(1, 4):
         pl.semaphore_signal(
             barrier, inc=1, device_id={"grp": lax.rem(group + i, 4)}, device_id_type=MESH
         )
-    for copy in loads[1:]:
-        copy.start()
+    for k in (1, 2, 3, 4, *range(6, 12)):
+        loads[k].start()
 
     def dense(raw, out):
         for index in np.ndindex(raw.shape[:-2]):
@@ -238,22 +239,37 @@
 
     loads[0].wait()
     dense(disp_raw, disp_ref)
+    loads[5].wait()
+    dense(samp_raw, samp_ref)
     pl.semaphore_wait(barrier, len(entry) + 3)
-    first_plane = pltpu.make_async_remote_copy(
-        src_ref=disp_ref.at[:, 0],
-        dst_ref=nb_first,
-        send_sem=first_sem.at[0],
-        recv_sem=first_sem.at[1],
-        device_id={"dev": lax.rem(me + 31, 32)},
-        device_id_type=MESH,
-    )
-    pl.when(me > 0)(first_plane.start)
+
+    lowest, highest = lax.rem(me, 8) == 0, lax.rem(me, 8) == 7
+    upper, lower = lowest & (me > 0), highest & (me < 31)
+    above, below = lax.rem(me + 1, 32), lax.rem(me + 31, 32)
+
+    def bordering(k, source, target, device):
+        return pltpu.make_async_remote_copy(
+            src_ref=source,
+            dst_ref=target,
+            send_sem=first_send.at[k],
+            recv_sem=first_recv.at[k],
+            device_id={"dev": device},
+            device_id_type=MESH,
+        )
+
+    first_plane = bordering(0, disp_ref.at[:, 0], nb_first, below)
+    last_planes = (
+        bordering(1, disp_ref.at[:, count - 1], nb_last, above),
+        bordering(2, samp_ref.at[count - 1], nb_mark, above),
+    )
+    pl.when(jnp.logical_not(lowest))(first_plane.start)
+    for copy in last_planes:
+        pl.when(lower)(copy.start)
     for peer in layer:
         pl.semaphore_signal(ready, inc=1, device_id={"dev": peer}, device_id_type=MESH)
-    for k in range(2, 6):
+    for k in range(2, 5):
         loads[k].wait()
     dense(force_raw, force_ref)
-    dense(samp_raw, samp_ref)
     for k, raw in enumerate((lame_raw, shear_raw)):
         wide = raw[...].astype(f32)
         for t in range(8):
@@ -315,44 +331,59 @@
                 wh[odd, rows, pl.ds(k * 256, 256)] = high[:, lanes]
                 wl[odd, rows, pl.ds(k * 256, 256)] = low[:, lanes]
 
-    one_hots, rows_high, rows_low = [], [], []
-    for plane in range(count):
-        sample = samp_ref[plane]
-        for s in range(8):
-            hit = jnp.broadcast_to(sample[s : s + 1], (32, 128)) == (
-                row_of((32, 128)) + group * 32
-            )
-            one_hots.append(jnp.where(hit, 1.0, 0.0).astype(bf16))
-    one_hot_ref[...] = jnp.concatenate(one_hots, axis=1)
+    def hot_of(sample, s, counted):
+        hit = jnp.broadcast_to(sample[s : s + 1], (32, 128)) == row_of((32, 128)) + group * 32
+        return jnp.where(hit, counted, 0.0).astype(bf16)
+
+    own_last = jnp.where(lower, 0.0, 1.0).astype(f32)
+    one_hot_ref[...] = jnp.concatenate(
+        [hot_of(samp_ref[p], s, (1.0, own_last)[p // (count - 1)]) for p in range(count) for s in range(8)],
+        axis=1,
+    )
     pl.semaphore_wait(ready, len(layer))
     everyone(lambda peer: mod_ref.at[peer], modbuf, mod_send, mod_recv)
     modbuf[me] = mod_ref[me]
 
-    pl.when(me < 31)(first_plane.wait_recv)
+    def sums_of(strain, one_hot):
+        n = strain[0].shape[0]
+        rows_high, rows_low = [], []
+        for p in range(n):
+            for c in range(6):
+                strainrow[p, pl.ds(c * 8, 8), :] = strain[c][p]
+        for p in range(n):
+            for s in range(8):
+                high, low = split(strainrow[p, pl.ds(s, 8, stride=8), :])
+                rows_high.append(high)
+                rows_low.append(low)
+
+        def against(rows):
+            return lax.dot_general(
+                one_hot,
+                jnp.concatenate(rows, axis=1),
+                (((1,), (1,)), ((), ())),
+                preferred_element_type=f32,
+            )
+
+        return against(rows_high) + against(rows_low)
+
+    pl.when(jnp.logical_not(highest))(first_plane.wait_recv)
     fields = [
-        jnp.concatenate([disp_ref[c], jnp.where(me < 31, nb_first[pl.ds(c, 1)], 0.0)], axis=0) for c in range(3)
+        jnp.concatenate([disp_ref[c], jnp.where(highest, 0.0, nb_first[pl.ds(c, 1)])], axis=0)
+        for c in range(3)
     ]
-    strain = strain_of(fields)
-    for plane in range(count):
-        for c in range(6):
-            strainrow[plane, pl.ds(c * 8, 8), :] = strain[c][plane]
-    for plane in range(count):
-        for s in range(8):
-            rows = strainrow[plane, pl.ds(s, 8, stride=8), :]
-            high, low = split(rows)
-            rows_high.append(high)
-            rows_low.append(low)
-    one_hot = one_hot_ref[...]
-
-    def against(rows):
-        return lax.dot_general(
-            one_hot,
-            jnp.concatenate(rows, axis=1),
-            (((1,), (1,)), ((), ())),
-            preferred_element_type=f32,
-        )
-
-    sums = against(rows_high) + against(rows_low)
+    sums_ref[:, pl.ds(0, 8)] = sums_of(strain_of(fields), one_hot_ref[...])
+
+    @pl.when(upper)
+    def _():
+        for copy in last_planes:
+            copy.wait_recv()
+        between = [
+            jnp.concatenate([nb_last[pl.ds(c, 1)], disp_ref[c, pl.ds(0, 1)]], axis=0) for c in range(3)
+        ]
+        hots = jnp.concatenate([hot_of(nb_mark, s, 1.0) for s in range(8)], axis=1)
+        sums_ref[:, pl.ds(0, 8)] += sums_of(strain_of(between), hots)
+
+    sums = sums_ref[:, pl.ds(0, 8)]
     for r in range(32):
         part[r, :, pl.ds(0, 8)] = sums[r : r + 1]
     everyone(lambda peer: part.at[peer], partbuf, part_send, part_recv)
@@ -714,7 +745,9 @@
             for q in range(4):
                 disp_out[c, p, pl.ds(q, 8, stride=4), :] = new[p][:, q * 32 : q * 32 + 32]
 
-    pl.when(me > 0)(first_plane.wait_send)
+    pl.when(jnp.logical_not(lowest))(first_plane.wait_send)
+    for copy in last_planes:
+        pl.when(lower)(copy.wait_send)
     for copy in near:
         copy.wait_send()
     for copy in rows_out:
@@ -779,6 +812,8 @@
             pltpu.VMEM((32, 16, 128), bf16),
             pltpu.VMEM((512, 128), f32),
             pltpu.VMEM((3, 8, 128), f32),
+            pltpu.VMEM((3, 8, 128), f32),
+            pltpu.VMEM((8, 128), jnp.int32),
             pltpu.VMEM((4,) + disp, f32),
             pltpu.VMEM((4,) + disp, f32),
             pltpu.VMEM((4,) + sample, jnp.int32),
@@ -787,6 +822,7 @@
             pltpu.VMEM((32, 1, 128), f32),
             pltpu.VMEM((count, 64, 128), f32),
             pltpu.VMEM((32, count * 1024), bf16),
+            pltpu.VMEM((32, 128), f32),
             *(pltpu.VMEM((2, HALF, HALF), bf16),) * 4,
             pltpu.VMEM((2, 256, 128), f32),
             pltpu.VMEM((3, 256, 128), f32),
@@ -797,7 +833,7 @@
             pltpu.VMEM((32, 1, 128), f32),
             pltpu.VMEM((1, 1, 128), f32),
             pltpu.VMEM((32, 1, 128), f32),
-            pltpu.SemaphoreType.REGULAR, dma((2,)), dma((3, 4)), dma((3, 4)), dma, dma, dma, dma,
+            pltpu.SemaphoreType.REGULAR, dma((3,)), dma((3,)), dma((3, 4)), dma((3, 4)), dma, dma, dma, dma,
             dma((3,)), dma((3,)), dma, dma, dma, dma, dma, dma,
         ],
         compiler_params=pltpu.CompilerParams(collective_id=0, has_side_effects=True, vmem_limit_bytes=24 << 20),

time: 34.5 us -> 33.7 us (0.977)
  Pallas kernels: 33.7 us -> 32.9 us
    pallas_call x1, Pallas kernels: 32.8 us -> 32 us  [shards(): pl.pallas_call(kernel, out_shape=(jax.ShapeDtypeStruct(displacement.shape...]
where the time goes in v6:
time: 33.7 us; the launch traced here: 33.5 us
  Pallas kernels  32.9 us (98%)
  between operations  0.64 us (2%)
    pallas_call x1, Pallas kernels, shards(): pl.pallas_call(kernel, out_shape=(jax.ShapeDtypeStruct(displacement.shape...  32 us
    pallas_call x1, Pallas kernels, shards(): pl.pallas_call(leave, out_shape=tuple((jax.ShapeDtypeStruct(a.shape, a.dt...  0.94 us

profile of v6, /device:TPU:1, one launch (start us, length us, event | category | flops | bytes accessed | tf_op | source)
XLA Modules:
  0.0 33.5 jit_solution(10047496770845379478)
XLA Ops:
  0.6 32.0 %shard_map.139 = (f32[3,2,32,32]{3,2,1,0:T(8,128)S(1)}, f32[1,8]{1,0:T(1,128)S(1)}, f32[1536,128]{1,0:T(8,128)S(1)}) custom-call(f32[3,2,32,32]{3,2,1,0:T(8,128)} %disp_in.1, f32[4,32,512]{2,1,0:T(8,128)} %constant.10.clone.wt_in, bf16[32,1024]{1,0:T(8,128)(2,1)} %bitcast.3, bf16[32,1024]{1,0:T(8,128)(2,1)} %bitcast.4, f32[3,2,32,32]{3,2,1,0:T(8,128)} %force_in.1, ...), custom_call_target="tpu_custom_call" | custom-call | tf_op jit(solution)/shard_map/pallas_call | solution.py:796
  32.6 0.9 %shard_map.140 = (f32[3,2,32,32]{3,2,1,0:T(8,128)}, f32[1,8]{1,0:T(1,128)}, f32[1536,128]{1,0:T(8,128)}) custom-call(f32[3,2,32,32]{3,2,1,0:T(8,128)S(1)} %get-tuple-element.9.a, f32[1,8]{1,0:T(1,128)S(1)} %get-tuple-element.10.b, f32[1536,128]{1,0:T(8,128)S(1)} %get-tuple-element.11.c), custom_call_target="tpu_custom_call" | custom-call | tf_op jit(solution)/shard_map/pallas_call | solution.py:842

commit v7 on v6

--- a/solution.py
+++ b/solution.py
@@ -27,7 +27,7 @@
 def tables():
     n = np.arange(VOX)
     theta = 2.0 * np.pi / VOX
-    order = np.concatenate([n[::2], n[1::2]])
+    order = np.concatenate([n[::4], n[2::4], n[1::2]])
     ky = np.repeat(order, 16)
     kz = np.tile(np.arange(16), VOX)
     yy = np.repeat(n[:16], VOX)
@@ -189,8 +189,8 @@
     disp_raw, wt_ref, lame_raw, shear_raw, force_raw, samp_raw, vt_ref, vz_ref, x_ref, spec_ref,
     steps_ref, slot_ref, in_sem,
     disp_ref, force_ref, samp_ref, mod_ref, modwide,
-    nb_first, nb_last, nb_mark, nb_disp, nb_force, nb_samp, modbuf, part, partbuf, strainrow, one_hot_ref, sums_ref,
-    wh, wl, vh, vl, field, disp_u, flu, flubuf,
+    nb_first, nb_last, nb_mark, nb, nb_samp, modbuf, part, partbuf, strainrow, one_hot_ref, sums_ref,
+    wh, wl, vh, vl, weh, wel, veh, vel, field, disp_u, flu, flubuf,
     rowbuf, joined, respbuf, moment, momentbuf,
     ready, first_send, first_recv, near_send, near_recv, mod_send, mod_recv, part_send, part_recv,
     y_send, y_recv, resp_send, resp_recv, flu_send, flu_recv, mom_send, mom_recv,
@@ -282,25 +282,31 @@
         strainrow[plane, pl.ds(48, 8), :] = jnp.ones((8, 128), f32)
         strainrow[plane, pl.ds(56, 8), :] = jnp.zeros((8, 128), f32)
 
+    places = {-1: (0, 6, 1), 1: (6, 6, 1 + count), 2: (12, 3, 1 + 2 * count), -2: (None, 0, 0)}
     near = []
-    for k, (source, target) in enumerate(
-        ((disp_ref, nb_disp), (force_ref, nb_force), (samp_ref, nb_samp))
-    ):
-        for o, offset in enumerate(NEAR):
-            if offset == 2 and k < 2:
-                continue
-            part_of = pl.ds(0 if offset == -2 else count - 1, 1) if abs(offset) == 2 else pl.ds(0, count)
-            index = (part_of,) if k == 2 else (slice(None), part_of)
+    for offset, (start, _, sample_start) in places.items():
+        device = lax.rem(me - offset + 32, 32)
+        plane = {2: 0, -2: count - 1}.get(offset)
+
+        def send(source, target, k, device=device):
             near.append(
                 pltpu.make_async_remote_copy(
-                    src_ref=source.at[index],
-                    dst_ref=target.at[(3 - o, *index)],
-                    send_sem=near_send.at[k, o],
-                    recv_sem=near_recv.at[k, 3 - o],
-                    device_id={"dev": lax.rem(me + offset + 32, 32)},
+                    src_ref=source,
+                    dst_ref=target,
+                    send_sem=near_send.at[k],
+                    recv_sem=near_recv.at[k],
+                    device_id={"dev": device},
                     device_id_type=MESH,
                 )
             )
+
+        width = count if plane is None else 1
+        cut_out = pl.ds(0 if plane is None else plane, width)
+        if start is not None:
+            for k, source in enumerate((disp_ref, force_ref)):
+                for c in range(3):
+                    send(source.at[c, cut_out], nb.at[pl.ds(k * 15 + start + c * width, width)], 0)
+        send(samp_ref.at[cut_out], nb_samp.at[pl.ds(sample_start, width)], 1)
 
     def everyone(source, target, send, recv):
         for peer in peers:
@@ -324,12 +330,18 @@
         c, s = wt_ref[0, pl.ds(y, 1), :], wt_ref[1, pl.ds(y, 1), :]
         zr, zi = wt_ref[2], wt_ref[3]
         rows = pl.ds(pl.multiple_of(y * 32, 32), 32)
-        for k, block in enumerate((c * zr + s * zi, c * zi - s * zr)):
-            high, low = split(block)
-            for odd in range(2):
-                lanes = slice(odd * 256, odd * 256 + 256)
-                wh[odd, rows, pl.ds(k * 256, 256)] = high[:, lanes]
-                wl[odd, rows, pl.ds(k * 256, 256)] = low[:, lanes]
+        blocks = [split(b) for b in (c * zr + s * zi, c * zi - s * zr)]
+        for k, (high, low) in enumerate(blocks):
+            wh[rows, pl.ds(k * 256, 256)] = high[:, 256:]
+            wl[rows, pl.ds(k * 256, 256)] = low[:, 256:]
+
+        @pl.when(y < 8)
+        def _():
+            for k, (high, low) in enumerate(blocks):
+                for q in range(2):
+                    lanes = slice(q * 128, q * 128 + 128)
+                    weh[q, rows, pl.ds(k * 128, 128)] = high[:, lanes]
+                    wel[q, rows, pl.ds(k * 128, 128)] = low[:, lanes]
 
     def hot_of(sample, s, counted):
         hit = jnp.broadcast_to(sample[s : s + 1], (32, 128)) == row_of((32, 128)) + group * 32
@@ -391,18 +403,27 @@
     for k in range(6, 12):
         loads[k].wait()
 
-    for odd in range(2):
-
-        @pl.loop(0, 16)
+    def back_rows(k, lanes):
+        row = pl.ds(k, 1)
+        c, s = vt_ref[0, row, pl.ds(0, lanes)], vt_ref[1, row, pl.ds(0, lanes)]
+        zr, zi = vz_ref[0, :, pl.ds(0, lanes)], vz_ref[1, :, pl.ds(0, lanes)]
+        return split(c * zr + s * zi), split(c * zi - s * zr)
+
+    @pl.loop(0, 16)
+    def _(k):
+        for p, (high, low) in enumerate(back_rows(16 + k, HALF)):
+            rows = pl.ds(pl.multiple_of(p * 256 + k * 16, 16), 16)
+            vh[rows, :] = high
+            vl[rows, :] = low
+
+    for q in range(2):
+
+        @pl.loop(0, 8)
         def _(k):
-            row = pl.ds(odd * 16 + k, 1)
-            c, s = vt_ref[0, row, :], vt_ref[1, row, :]
-            zr, zi = vz_ref[0], vz_ref[1]
-            for p, block in enumerate((c * zr + s * zi, c * zi - s * zr)):
-                rows = pl.ds(pl.multiple_of(p * 256 + k * 16, 16), 16)
-                high, low = split(block)
-                vh[odd, rows, :] = high
-                vl[odd, rows, :] = low
+            for p, (high, low) in enumerate(back_rows(q * 8 + k, 256)):
+                rows = pl.ds(pl.multiple_of(p * 128 + k * 16, 16), 16)
+                veh[q, rows, :] = high
+                vel[q, rows, :] = low
 
     ref = modbuf.at[pl.ds(0, 31)]
     pltpu.make_async_copy(ref, ref, mod_recv).wait()
@@ -432,14 +453,22 @@
             ],
             axis=1,
         )
-        halves = [rows[:, :HALF] + rows[:, HALF:], rows[:, :HALF] - rows[:, HALF:]]
-        sides = []
-        for odd, half in enumerate(halves):
-            high, low = split(half)
-            both = mm(jnp.concatenate([high, low], axis=0), wh[odd])
-            sides.append(both[:64] + (both[64:] + mm(high, wl[odd])))
+        even, odd = rows[:, :HALF] + rows[:, HALF:], rows[:, :HALF] - rows[:, HALF:]
+
+        def part_of(data, high_ref, low_ref):
+            high, low = split(data)
+            both = mm(jnp.concatenate([high, low], axis=0), high_ref[...])
+            return both[:64] + (both[64:] + mm(high, low_ref[...]))
+
+        sides = [
+            part_of(even[:, :256] + even[:, 256:], weh.at[0], wel.at[0]),
+            part_of(even[:, :256] - even[:, 256:], weh.at[1], wel.at[1]),
+            part_of(odd, wh, wl),
+        ]
         plane = jnp.concatenate(
-            [sides[0][:, :256], sides[1][:, :256], sides[0][:, 256:], sides[1][:, 256:]], axis=1
+            [side[:, : side.shape[1] // 2] for side in sides]
+            + [side[:, side.shape[1] // 2 :] for side in sides],
+            axis=1,
         )
         stacked = jnp.concatenate(
             [
@@ -452,8 +481,6 @@
 
     ref = partbuf.at[pl.ds(0, 31)]
     pltpu.make_async_copy(ref, ref, part_recv).wait()
-    for copy in near:
-        copy.start()
     total = jnp.sum(partbuf[...], axis=0)
     lane1 = lane_of((1, 128))
 
@@ -504,21 +531,24 @@
         axis=0,
     )
     back = product(x_ref[1], mixed)
-    sides = []
-    for odd in range(2):
+    def side_of(start, width, high_ref, low_ref):
         lines = jnp.concatenate(
             [
                 jnp.concatenate(
-                    [back[h : h + 32, c * HALF + odd * 256 :][:, :256] for h in (0, 32)], axis=1
+                    [back[h : h + 32, c * HALF + start :][:, :width] for h in (0, 32)], axis=1
                 )
                 for c in range(3)
             ],
             axis=0,
         )
         high, low = split(lines)
-        both = mm(jnp.concatenate([high, low], axis=0), vh[odd])
-        sides.append(both[:96] + (both[96:] + mm(high, vl[odd])))
-    space = jnp.concatenate([sides[0] + sides[1], sides[0] - sides[1]], axis=1)
+        both = mm(jnp.concatenate([high, low], axis=0), high_ref[...])
+        return both[:96] + (both[96:] + mm(high, low_ref[...]))
+
+    first, second = (side_of(q * 128, 128, veh.at[q], vel.at[q]) for q in range(2))
+    even = jnp.concatenate([first + second, first - second], axis=1)
+    odd = side_of(256, 256, vh, vl)
+    space = jnp.concatenate([even + odd, even - odd], axis=1)
     for c in range(3):
         for s in range(8):
             disp_u[c, pl.ds(s, 32, stride=8), :] = space[
@@ -571,52 +601,49 @@
         own_row = own_row + jnp.where(lane1 == group * 16 + 8 + c, load[c], 0.0)
 
     rowbuf[3] = own_row
-    rows_out = []
     for i in range(1, 4):
-        rows_out.append(
+        (
             pltpu.make_async_remote_copy(
                 src_ref=rowbuf.at[3],
                 dst_ref=rowbuf.at[i - 1],
-                send_sem=y_send.at[i - 1],
-                recv_sem=y_recv.at[i - 1],
+                send_sem=y_send,
+                recv_sem=y_recv,
                 device_id={"grp": lax.rem(group + i, 4)},
                 device_id_type=MESH,
             )
-        )
-        rows_out[-1].start()
-    for copy in rows_out:
-        copy.wait_recv()
+        ).start()
+    arrived = rowbuf.at[pl.ds(0, 3)]
+    for copy in near:
+        copy.start()
+    pltpu.make_async_copy(arrived, arrived, y_recv).wait()
     joined[0] = rowbuf[0] + rowbuf[1] + rowbuf[2] + rowbuf[3]
     everyone(lambda peer: joined.at[0], respbuf, resp_send, resp_recv)
     respbuf[me] = joined[0]
     everyone(lambda peer: flu.at[peer], flubuf, flu_send, flu_recv)
     flubuf[me] = flu[me]
 
-    for copy in near:
-        copy.wait_recv()
+    pltpu.make_async_copy(nb, nb, near_recv.at[0]).wait()
+    pltpu.make_async_copy(nb_samp, nb_samp, near_recv.at[1]).wait()
     exists = [(me * count + j >= 3).astype(f32) * (me * count + j < 67).astype(f32) for j in range(8)]
 
-    def extended(own, near_ref, c):
-        def get(ref, p):
-            return ref[c, pl.ds(p, 1)] if c is not None else ref[pl.ds(p, 1)]
-
-        lowest = get(near_ref.at[0], 1) if c is None else get(near_ref.at[1], 0)
-        planes = [lowest, get(near_ref.at[1], 0), get(near_ref.at[1], 1)]
-        planes += [get(own, 0), get(own, 1)]
-        planes += [get(near_ref.at[2], 0), get(near_ref.at[2], 1), get(near_ref.at[3], 0)]
-        return planes
+    def around_of(own, k, c):
+        below = [nb[pl.ds(k * 15 + c * 2 + p, 1)] for p in (0, 0, 1)]
+        above = [nb[pl.ds(k * 15 + 6 + c * 2 + p, 1)] for p in range(2)]
+        return [*below, own[c, pl.ds(0, 1)], own[c, pl.ds(1, 1)], *above, nb[pl.ds(k * 15 + 12 + c, 1)]]
 
     def masked(planes):
         return jnp.concatenate([p * m for p, m in zip(planes, exists)], axis=0)
 
-    around = [masked(extended(disp_ref, nb_disp, c)) for c in range(3)]
-    outside = [masked(extended(force_ref, nb_force, c)) for c in range(3)]
+    around = [masked(around_of(disp_ref, 0, c)) for c in range(3)]
+    outside = [masked(around_of(force_ref, 1, c)) for c in range(3)]
     given = [
         (outside[c][1:] - spring_rate * around[c][1:])
         * jnp.concatenate([jnp.full((1, 8, 128), m) for m in exists[1:]], axis=0)
         for c in range(3)
     ]
-    samples = extended(samp_ref, nb_samp, None)
+    samples = [nb_samp[pl.ds(j, 1)] for j in range(3)]
+    samples += [samp_ref[pl.ds(p, 1)] for p in range(2)]
+    samples += [nb_samp[pl.ds(j, 1)] for j in range(3, 6)]
 
     all_arrived(respbuf, resp_recv)
     gathered = jnp.concatenate([respbuf[r] for r in range(32)], axis=0)
@@ -748,10 +775,9 @@
     pl.when(jnp.logical_not(lowest))(first_plane.wait_send)
     for copy in last_planes:
         pl.when(lower)(copy.wait_send)
-    for copy in near:
-        copy.wait_send()
-    for copy in rows_out:
-        copy.wait_send()
+    pltpu.make_async_copy(nb, nb, near_send.at[0]).wait()
+    pltpu.make_async_copy(nb_samp, nb_samp, near_send.at[1]).wait()
+    pltpu.make_async_copy(arrived, arrived, y_send).wait()
     for buffer, sem in (
         (modbuf, mod_send), (partbuf, part_send), (respbuf, resp_send),
         (flubuf, flu_send), (momentbuf, mom_send),
@@ -814,16 +840,16 @@
             pltpu.VMEM((3, 8, 128), f32),
             pltpu.VMEM((3, 8, 128), f32),
             pltpu.VMEM((8, 128), jnp.int32),
-            pltpu.VMEM((4,) + disp, f32),
-            pltpu.VMEM((4,) + disp, f32),
-            pltpu.VMEM((4,) + sample, jnp.int32),
+            pltpu.VMEM((30, 8, 128), f32),
+            pltpu.VMEM((6, 8, 128), jnp.int32),
             pltpu.VMEM((32, 16, 128), bf16),
             pltpu.VMEM((32, 1, 128), f32),
             pltpu.VMEM((32, 1, 128), f32),
             pltpu.VMEM((count, 64, 128), f32),
             pltpu.VMEM((32, count * 1024), bf16),
             pltpu.VMEM((32, 128), f32),
-            *(pltpu.VMEM((2, HALF, HALF), bf16),) * 4,
+            *(pltpu.VMEM((HALF, HALF), bf16),) * 4,
+            *(pltpu.VMEM((2, 256, 256), bf16),) * 4,
             pltpu.VMEM((2, 256, 128), f32),
             pltpu.VMEM((3, 256, 128), f32),
             pltpu.VMEM((32, 48, 128), wire),
@@ -833,8 +859,8 @@
             pltpu.VMEM((32, 1, 128), f32),
             pltpu.VMEM((1, 1, 128), f32),
             pltpu.VMEM((32, 1, 128), f32),
-            pltpu.SemaphoreType.REGULAR, dma((3,)), dma((3,)), dma((3, 4)), dma((3, 4)), dma, dma, dma, dma,
-            dma((3,)), dma((3,)), dma, dma, dma, dma, dma, dma,
+            pltpu.SemaphoreType.REGULAR, dma((3,)), dma((3,)), dma((2,)), dma((2,)), dma, dma, dma, dma,
+            dma, dma, dma, dma, dma, dma, dma, dma,
         ],
         compiler_params=pltpu.CompilerParams(collective_id=0, has_side_effects=True, vmem_limit_bytes=24 << 20),
     )(*[pltpu.with_memory_space_constraint(a, pltpu.HBM) for a in operands + scalars])

time: 33.7 us -> 33.3 us (0.988)
  no operation moved by 1% of the time
where the time goes in v7:
time: 33.3 us; the launch traced here: 33.2 us
  Pallas kernels  32.6 us (98%)
  between operations  0.64 us (2%)
    pallas_call x1, Pallas kernels, shards(): pl.pallas_call(kernel, out_shape=(jax.ShapeDtypeStruct(displacement.shape...  31.6 us
    pallas_call x1, Pallas kernels, shards(): pl.pallas_call(leave, out_shape=tuple((jax.ShapeDtypeStruct(a.shape, a.dt...  0.94 us

profile of v7, /device:TPU:1, one launch (start us, length us, event | category | flops | bytes accessed | tf_op | source)
XLA Modules:
  0.0 33.2 jit_solution(2661586590267003569)
XLA Ops:
  0.6 31.6 %shard_map.139 = (f32[3,2,32,32]{3,2,1,0:T(8,128)S(1)}, f32[1,8]{1,0:T(1,128)S(1)}, f32[1536,128]{1,0:T(8,128)S(1)}) custom-call(f32[3,2,32,32]{3,2,1,0:T(8,128)} %disp_in.1, f32[4,32,512]{2,1,0:T(8,128)} %constant.10.clone.wt_in, bf16[32,1024]{1,0:T(8,128)(2,1)} %bitcast.3, bf16[32,1024]{1,0:T(8,128)(2,1)} %bitcast.4, f32[3,2,32,32]{3,2,1,0:T(8,128)} %force_in.1, ...), custom_call_target="tpu_custom_call" | custom-call | tf_op jit(solution)/shard_map/pallas_call | solution.py:822
  32.3 0.9 %shard_map.140 = (f32[3,2,32,32]{3,2,1,0:T(8,128)}, f32[1,8]{1,0:T(1,128)}, f32[1536,128]{1,0:T(8,128)}) custom-call(f32[3,2,32,32]{3,2,1,0:T(8,128)S(1)} %get-tuple-element.9.a, f32[1,8]{1,0:T(1,128)S(1)} %get-tuple-element.10.b, f32[1536,128]{1,0:T(8,128)S(1)} %get-tuple-element.11.c), custom_call_target="tpu_custom_call" | custom-call | tf_op jit(solution)/shard_map/pallas_call | solution.py:868

commit v8 on v7

--- a/solution.py
+++ b/solution.py
@@ -179,7 +179,7 @@
     scale = jnp.ones_like(mu)
     for rate in rates:
         f = base * scale * scale
-        scale = scale * (1.0 - rate * (f / (1.0 + f)))
+        scale = scale * ((1.0 - rate) + rate / (1.0 + f))
     return scale, base * scale * scale
 
 
@@ -479,6 +479,9 @@
         )
         return product(x_ref[0], stacked)
 
+    lame, shear = moduli(0, 32)
+    field[0] = (lame + (2.0 / 3.0) * shear).reshape(256, 128)
+
     ref = partbuf.at[pl.ds(0, 31)]
     pltpu.make_async_copy(ref, ref, part_recv).wait()
     total = jnp.sum(partbuf[...], axis=0)
@@ -495,13 +498,9 @@
     rates = [jnp.where(k < own_steps, relax_rate, 0.0).astype(f32) for k in range(KMAX)]
     size = norm_of(d)
 
-    @pl.loop(0, 4)
-    def _(t):
-        lame, shear = moduli(t * 8, 8)
-        field[0, at(t * 8, 8), :] = (lame + (2.0 / 3.0) * shear).reshape(64, 128)
-        scale, _ = relaxed(shear, size, rates)
-        field[1, at(t * 8, 8), :] = (2.0 * shear * scale).reshape(64, 128)
-
+    _, shear = moduli(0, 32)
+    scale, _ = relaxed(shear, size, rates)
+    field[1] = (2.0 * shear * scale).reshape(256, 128)
     spectrum = forward()
     spectrum_a, spectrum_b = spectrum[:, :HALF], spectrum[:, HALF:]
     mix = d[0] * spec_ref[1]

time: 33.3 us -> 33.2 us (level)
  no operation moved by 1% of the time
where the time goes in v8:
time: 33.2 us; the launch traced here: 33.1 us
  Pallas kernels  32.4 us (98%)
  between operations  0.64 us (2%)
    pallas_call x1, Pallas kernels, shards(): pl.pallas_call(kernel, out_shape=(jax.ShapeDtypeStruct(displacement.shape...  31.5 us
    pallas_call x1, Pallas kernels, shards(): pl.pallas_call(leave, out_shape=tuple((jax.ShapeDtypeStruct(a.shape, a.dt...  0.94 us

profile of v8, /device:TPU:1, one launch (start us, length us, event | category | flops | bytes accessed | tf_op | source)
XLA Modules:
  0.0 33.1 jit_solution(9652956512238065312)
XLA Ops:
  0.6 31.5 %shard_map.139 = (f32[3,2,32,32]{3,2,1,0:T(8,128)S(1)}, f32[1,8]{1,0:T(1,128)S(1)}, f32[1536,128]{1,0:T(8,128)S(1)}) custom-call(f32[3,2,32,32]{3,2,1,0:T(8,128)} %disp_in.1, f32[4,32,512]{2,1,0:T(8,128)} %constant.10.clone.wt_in, bf16[32,1024]{1,0:T(8,128)(2,1)} %bitcast.3, bf16[32,1024]{1,0:T(8,128)(2,1)} %bitcast.4, f32[3,2,32,32]{3,2,1,0:T(8,128)} %force_in.1, ...), custom_call_target="tpu_custom_call" | custom-call | tf_op jit(solution)/shard_map/pallas_call | solution.py:821
  32.1 0.9 %shard_map.140 = (f32[3,2,32,32]{3,2,1,0:T(8,128)}, f32[1,8]{1,0:T(1,128)}, f32[1536,128]{1,0:T(8,128)}) custom-call(f32[3,2,32,32]{3,2,1,0:T(8,128)S(1)} %get-tuple-element.9.a, f32[1,8]{1,0:T(1,128)S(1)} %get-tuple-element.10.b, f32[1536,128]{1,0:T(8,128)S(1)} %get-tuple-element.11.c), custom_call_target="tpu_custom_call" | custom-call | tf_op jit(solution)/shard_map/pallas_call | solution.py:867

commit v9 on v8

--- a/solution.py
+++ b/solution.py
@@ -189,7 +189,7 @@
     disp_raw, wt_ref, lame_raw, shear_raw, force_raw, samp_raw, vt_ref, vz_ref, x_ref, spec_ref,
     steps_ref, slot_ref, in_sem,
     disp_ref, force_ref, samp_ref, mod_ref, modwide,
-    nb_first, nb_last, nb_mark, nb, nb_samp, modbuf, part, partbuf, strainrow, one_hot_ref, sums_ref,
+    nb_first, nb_last, nb_mark, nb, nb_samp, sized, modbuf, partbuf, strainrow, one_hot_ref, sums_ref,
     wh, wl, vh, vl, weh, wel, veh, vel, field, disp_u, flu, flubuf,
     rowbuf, joined, respbuf, moment, momentbuf,
     ready, first_send, first_recv, near_send, near_recv, mod_send, mod_recv, part_send, part_recv,
@@ -277,7 +277,7 @@
     for r in range(32):
         mod_ref[r] = modwide[pl.ds(r * 16, 16), :].astype(bf16)
 
-    part[...] = jnp.zeros_like(part)
+    sums_ref[...] = jnp.zeros_like(sums_ref)
     for plane in range(count):
         strainrow[plane, pl.ds(48, 8), :] = jnp.ones((8, 128), f32)
         strainrow[plane, pl.ds(56, 8), :] = jnp.zeros((8, 128), f32)
@@ -312,7 +312,7 @@
         for peer in peers:
             pltpu.make_async_remote_copy(
                 src_ref=source(peer),
-                dst_ref=target.at[me],
+                dst_ref=target.at[me] if len(target.shape) == 3 else target.at[pl.ds(me, 1)],
                 send_sem=send,
                 recv_sem=recv,
                 device_id={"dev": peer},
@@ -320,7 +320,7 @@
             ).start()
 
     def all_arrived(target, recv):
-        ref = target.at[pl.ds(0, 31)]
+        ref = target.at[pl.ds(0, 31)] if len(target.shape) == 3 else sized.at[pl.ds(0, 31)]
         pltpu.make_async_copy(ref, ref, recv).wait()
 
     loads[1].wait()
@@ -395,11 +395,8 @@
         hots = jnp.concatenate([hot_of(nb_mark, s, 1.0) for s in range(8)], axis=1)
         sums_ref[:, pl.ds(0, 8)] += sums_of(strain_of(between), hots)
 
-    sums = sums_ref[:, pl.ds(0, 8)]
-    for r in range(32):
-        part[r, :, pl.ds(0, 8)] = sums[r : r + 1]
-    everyone(lambda peer: part.at[peer], partbuf, part_send, part_recv)
-    partbuf[me] = part[me]
+    everyone(lambda peer: sums_ref.at[pl.ds(peer, 1)], partbuf, part_send, part_recv)
+    partbuf[pl.ds(me, 1), :] = sums_ref[pl.ds(me, 1), :]
     for k in range(6, 12):
         loads[k].wait()
 
@@ -482,9 +479,8 @@
     lame, shear = moduli(0, 32)
     field[0] = (lame + (2.0 / 3.0) * shear).reshape(256, 128)
 
-    ref = partbuf.at[pl.ds(0, 31)]
-    pltpu.make_async_copy(ref, ref, part_recv).wait()
-    total = jnp.sum(partbuf[...], axis=0)
+    all_arrived(partbuf, part_recv)
+    total = jnp.sum(partbuf[...], axis=0, keepdims=True)
     lane1 = lane_of((1, 128))
 
     def pick(row, k):
@@ -617,7 +613,7 @@
     pltpu.make_async_copy(arrived, arrived, y_recv).wait()
     joined[0] = rowbuf[0] + rowbuf[1] + rowbuf[2] + rowbuf[3]
     everyone(lambda peer: joined.at[0], respbuf, resp_send, resp_recv)
-    respbuf[me] = joined[0]
+    respbuf[pl.ds(me, 1), :] = joined[0]
     everyone(lambda peer: flu.at[peer], flubuf, flu_send, flu_recv)
     flubuf[me] = flu[me]
 
@@ -645,8 +641,7 @@
     samples += [nb_samp[pl.ds(j, 1)] for j in range(3, 6)]
 
     all_arrived(respbuf, resp_recv)
-    gathered = jnp.concatenate([respbuf[r] for r in range(32)], axis=0)
-    gathered = jnp.concatenate([gathered, jnp.zeros((96, 128), f32)], axis=0).T
+    gathered = jnp.concatenate([respbuf[...], jnp.zeros((96, 128), f32)], axis=0).T
     cells = []
     for c in range(8):
         row = jnp.concatenate(
@@ -708,11 +703,11 @@
     column = jnp.sum(jnp.concatenate(rows, axis=0), axis=1, keepdims=True)
     moment[0] = jnp.sum(jnp.where(lane8 == row8, column, 0.0), axis=0, keepdims=True)
     everyone(lambda peer: moment.at[0], momentbuf, mom_send, mom_recv)
-    momentbuf[me] = moment[0]
+    momentbuf[pl.ds(me, 1), :] = moment[0]
 
     def owner(r, acc):
         taken = jnp.where(slot_ref[group * 32 + r] == me, 1.0, 0.0).astype(f32)
-        return acc + taken * respbuf[r]
+        return acc + taken * respbuf[pl.ds(r, 1), :]
 
     row = lax.fori_loop(0, 32, owner, jnp.zeros((1, 128), f32))
     shifted = jnp.zeros((1, 128), f32)
@@ -721,7 +716,7 @@
         shifted = shifted + here * roll(row, -16 * g, 1)
     row_out[...] = shifted[:, :8]
 
-    table = jnp.concatenate([respbuf[r] for r in range(32)], axis=0)
+    table = respbuf[...]
     lane32 = lane_of((32, 128))
     group_load = [
         jnp.sum(jnp.where(lane32 == group * 16 + 8 + c, table, 0.0), axis=1, keepdims=True)
@@ -736,7 +731,7 @@
             )
 
     all_arrived(momentbuf, mom_recv)
-    total = jnp.sum(momentbuf[...], axis=0)
+    total = jnp.sum(momentbuf[...], axis=0, keepdims=True)
     m = [pick(total, k) for k in range(6)]
 
     def form(a, b, first):
@@ -781,8 +776,7 @@
         (modbuf, mod_send), (partbuf, part_send), (respbuf, resp_send),
         (flubuf, flu_send), (momentbuf, mom_send),
     ):
-        ref = buffer.at[pl.ds(0, 31)]
-        pltpu.make_async_copy(ref, ref, sem).wait()
+        all_arrived(buffer, sem)
 
 
 def leave(a, b, c, a_out, b_out, c_out, sem):
@@ -841,9 +835,9 @@
             pltpu.VMEM((8, 128), jnp.int32),
             pltpu.VMEM((30, 8, 128), f32),
             pltpu.VMEM((6, 8, 128), jnp.int32),
+            pltpu.VMEM((32, 1, 128), f32),
             pltpu.VMEM((32, 16, 128), bf16),
-            pltpu.VMEM((32, 1, 128), f32),
-            pltpu.VMEM((32, 1, 128), f32),
+            pltpu.VMEM((32, 128), f32),
             pltpu.VMEM((count, 64, 128), f32),
             pltpu.VMEM((32, count * 1024), bf16),
             pltpu.VMEM((32, 128), f32),
@@ -855,9 +849,9 @@
             pltpu.VMEM((32, 48, 128), wire),
             pltpu.VMEM((4, 1, 128), f32),
             pltpu.VMEM((1, 1, 128), f32),
-            pltpu.VMEM((32, 1, 128), f32),
+            pltpu.VMEM((32, 128), f32),
             pltpu.VMEM((1, 1, 128), f32),
-            pltpu.VMEM((32, 1, 128), f32),
+            pltpu.VMEM((32, 128), f32),
             pltpu.SemaphoreType.REGULAR, dma((3,)), dma((3,)), dma((2,)), dma((2,)), dma, dma, dma, dma,
             dma, dma, dma, dma, dma, dma, dma, dma,
         ],

time: 33.2 us -> 33.1 us (level)
  no operation moved by 1% of the time
where the time goes in v9:
time: 33.1 us; the launch traced here: 33 us
  Pallas kernels  32.4 us (98%)
  between operations  0.64 us (2%)
    pallas_call x1, Pallas kernels, shards(): pl.pallas_call(kernel, out_shape=(jax.ShapeDtypeStruct(displacement.shape...  31.4 us
    pallas_call x1, Pallas kernels, shards(): pl.pallas_call(leave, out_shape=tuple((jax.ShapeDtypeStruct(a.shape, a.dt...  0.94 us

profile of v9, /device:TPU:1, one launch (start us, length us, event | category | flops | bytes accessed | tf_op | source)
XLA Modules:
  0.0 33.0 jit_solution(13577420344780730617)
XLA Ops:
  0.6 31.4 %shard_map.139 = (f32[3,2,32,32]{3,2,1,0:T(8,128)S(1)}, f32[1,8]{1,0:T(1,128)S(1)}, f32[1536,128]{1,0:T(8,128)S(1)}) custom-call(f32[3,2,32,32]{3,2,1,0:T(8,128)} %disp_in.1, f32[4,32,512]{2,1,0:T(8,128)} %constant.10.clone.wt_in, bf16[32,1024]{1,0:T(8,128)(2,1)} %bitcast.3, bf16[32,1024]{1,0:T(8,128)(2,1)} %bitcast.4, f32[3,2,32,32]{3,2,1,0:T(8,128)} %force_in.1, ...), custom_call_target="tpu_custom_call" | custom-call | tf_op jit(solution)/shard_map/pallas_call | solution.py:815
  32.0 0.9 %shard_map.140 = (f32[3,2,32,32]{3,2,1,0:T(8,128)}, f32[1,8]{1,0:T(1,128)}, f32[1536,128]{1,0:T(8,128)}) custom-call(f32[3,2,32,32]{3,2,1,0:T(8,128)S(1)} %get-tuple-element.9.a, f32[1,8]{1,0:T(1,128)S(1)} %get-tuple-element.10.b, f32[1536,128]{1,0:T(8,128)S(1)} %get-tuple-element.11.c), custom_call_target="tpu_custom_call" | custom-call | tf_op jit(solution)/shard_map/pallas_call | solution.py:861

commit v10 on v9

--- a/solution.py
+++ b/solution.py
@@ -308,8 +308,8 @@
                     send(source.at[c, cut_out], nb.at[pl.ds(k * 15 + start + c * width, width)], 0)
         send(samp_ref.at[cut_out], nb_samp.at[pl.ds(sample_start, width)], 1)
 
-    def everyone(source, target, send, recv):
-        for peer in peers:
+    def everyone(source, target, send, recv, some=None):
+        for peer in peers if some is None else some:
             pltpu.make_async_remote_copy(
                 src_ref=source(peer),
                 dst_ref=target.at[me] if len(target.shape) == 3 else target.at[pl.ds(me, 1)],
@@ -322,6 +322,12 @@
     def all_arrived(target, recv):
         ref = target.at[pl.ds(0, 31)] if len(target.shape) == 3 else sized.at[pl.ds(0, 31)]
         pltpu.make_async_copy(ref, ref, recv).wait()
+
+    known = [k for k, (a, b, c) in enumerate(OTHERS) if a == 0 or (b, c) == (0, 0)]
+    unknown = [peer for k, peer in enumerate(peers) if k not in known]
+    everyone(
+        lambda peer: mod_ref.at[peer], modbuf, mod_send, mod_recv, [peers[k] for k in known]
+    )
 
     loads[1].wait()
 
@@ -353,7 +359,7 @@
         axis=1,
     )
     pl.semaphore_wait(ready, len(layer))
-    everyone(lambda peer: mod_ref.at[peer], modbuf, mod_send, mod_recv)
+    everyone(lambda peer: mod_ref.at[peer], modbuf, mod_send, mod_recv, unknown)
     modbuf[me] = mod_ref[me]
 
     def sums_of(strain, one_hot):

time: 33.1 us -> 34.1 us (1.030)
  Pallas kernels: 32.4 us -> 33.3 us
    pallas_call x1, Pallas kernels: 31.4 us -> 32.4 us  [shards(): pl.pallas_call(kernel, out_shape=(jax.ShapeDtypeStruct(displacement.shape...]
where the time goes in v10:
time: 34.1 us; the launch traced here: 33.9 us
  Pallas kernels  33.3 us (98%)
  between operations  0.64 us (2%)
    pallas_call x1, Pallas kernels, shards(): pl.pallas_call(kernel, out_shape=(jax.ShapeDtypeStruct(displacement.shape...  32.4 us
    pallas_call x1, Pallas kernels, shards(): pl.pallas_call(leave, out_shape=tuple((jax.ShapeDtypeStruct(a.shape, a.dt...  0.94 us

profile of v10, /device:TPU:1, one launch (start us, length us, event | category | flops | bytes accessed | tf_op | source)
XLA Modules:
  0.0 33.9 jit_solution(18320831989952565959)
XLA Ops:
  0.6 32.4 %shard_map.139 = (f32[3,2,32,32]{3,2,1,0:T(8,128)S(1)}, f32[1,8]{1,0:T(1,128)S(1)}, f32[1536,128]{1,0:T(8,128)S(1)}) custom-call(f32[3,2,32,32]{3,2,1,0:T(8,128)} %disp_in.1, f32[4,32,512]{2,1,0:T(8,128)} %constant.10.clone.wt_in, bf16[32,1024]{1,0:T(8,128)(2,1)} %bitcast.3, bf16[32,1024]{1,0:T(8,128)(2,1)} %bitcast.4, f32[3,2,32,32]{3,2,1,0:T(8,128)} %force_in.1, ...), custom_call_target="tpu_custom_call" | custom-call | tf_op jit(solution)/shard_map/pallas_call | solution.py:821
  33.0 0.9 %shard_map.140 = (f32[3,2,32,32]{3,2,1,0:T(8,128)}, f32[1,8]{1,0:T(1,128)}, f32[1536,128]{1,0:T(8,128)}) custom-call(f32[3,2,32,32]{3,2,1,0:T(8,128)S(1)} %get-tuple-element.9.a, f32[1,8]{1,0:T(1,128)S(1)} %get-tuple-element.10.b, f32[1536,128]{1,0:T(8,128)S(1)} %get-tuple-element.11.c), custom_call_target="tpu_custom_call" | custom-call | tf_op jit(solution)/shard_map/pallas_call | solution.py:867
